TPU v7x, 8 devices: a whole 2x2x1 slice. The times are simulated.
8 devices in a mesh: rep: 1 (over z), ep: 8 (over y, x, core).
Axes of the slice: x: 2, y: 2, z: 1, core: 2. Of those that a mesh axis runs over, the one named last changes fastest.
Arguments:
- x: bfloat16 [1024, 2048], P(('rep', 'ep'))
- cache: bfloat16 [1024, 256, 576], P(('rep', 'ep'))
- lens: int32 [1024], P(('rep', 'ep'))
- ids: int32 [1024, 6], P(('rep', 'ep'))
- rw: float32 [1024, 6], P(('rep', 'ep'))
- w_q: bfloat16 [2048, 3072], replicated
- w_dkv: bfloat16 [2048, 576], replicated
- w_uk: bfloat16 [16, 128, 512], replicated
- w_uv: bfloat16 [16, 512, 128], replicated
- w_o: bfloat16 [2048, 2048], replicated
- s_gate: bfloat16 [2048, 2816], replicated
- s_up: bfloat16 [2048, 2816], replicated
- s_down: bfloat16 [2816, 2048], replicated
- e_gate: bfloat16 [64, 2048, 1408], P('ep')
- e_up: bfloat16 [64, 2048, 1408], P('ep')
- e_down: bfloat16 [64, 1408, 2048], P('ep')
Outputs:
- output 1: bfloat16 [1024, 2048], P(('rep', 'ep'))
- output 2: bfloat16 [1024, 576], P(('rep', 'ep'))
All inputs are finite; a program needn't handle non-finite values.
Results may differ from a plain program's by a relative error of at most 0.0118949.
Values are sent between devices in bfloat16 or wider.
A program may use at most 1 GiB of HBM per device.

v0:
```python
import jax
import jax.numpy as jnp
from jax import lax
from jax.sharding import PartitionSpec as P, NamedSharding

EPS = 1e-6
ROPE_BASE = 1.0e4
CAP_FACTOR = 2


def rms(v):
    v = v.astype(jnp.float32)
    return v * lax.rsqrt(jnp.mean(v * v, axis=-1, keepdims=True) + EPS)


def rope(v, pos):
    half = v.shape[-1] // 2
    inv = ROPE_BASE ** (-2.0 * jnp.arange(half, dtype=jnp.float32) / v.shape[-1])
    ang = pos.astype(jnp.float32)[..., None] * inv
    cs = jnp.cos(ang)
    sn = jnp.sin(ang)
    v1 = v[..., :half]
    v2 = v[..., half:]
    return jnp.concatenate([v1 * cs - v2 * sn, v2 * cs + v1 * sn], axis=-1)


def swiglu(u, wg, wu, wd):
    g = jnp.dot(u, wg, preferred_element_type=jnp.float32)
    v = jnp.dot(u, wu, preferred_element_type=jnp.float32)
    return jnp.dot((jax.nn.silu(g) * v).astype(jnp.bfloat16), wd, preferred_element_type=jnp.float32)


def route(col, w, n_col, cap):
    bsz, top = col.shape
    hit = (col[:, :, None] == jnp.arange(n_col)[None, None, :]).astype(jnp.bfloat16)
    flat = hit.reshape(bsz * top, n_col)
    idx = jnp.arange(bsz * top)
    low = (idx[:, None] > idx[None, :]).astype(jnp.bfloat16)
    before = jnp.dot(low, flat, preferred_element_type=jnp.float32)
    rank = jnp.sum(before * flat.astype(jnp.float32), axis=1).astype(jnp.int32).reshape(bsz, top)
    at = (rank[:, :, None] == jnp.arange(cap)[None, None, :]).astype(jnp.bfloat16)
    disp = jnp.einsum('bke,bkr->ber', hit, at, preferred_element_type=jnp.float32).astype(jnp.bfloat16).reshape(bsz, n_col * cap)
    w = w.astype(jnp.float32)
    w1 = w.astype(jnp.bfloat16)
    r1 = w - w1.astype(jnp.float32)
    w2 = r1.astype(jnp.bfloat16)
    w3 = (r1 - w2.astype(jnp.float32)).astype(jnp.bfloat16)
    hw = jnp.stack([w1, w2, w3])[:, :, :, None] * hit[None]
    comb = jnp.einsum('jbke,bkr->jber', hw, at, preferred_element_type=jnp.float32).astype(jnp.bfloat16).reshape(-1, n_col * cap)
    return disp, comb


def attention(x, cache, lens, w_q, w_dkv, w_uk, w_uv, w_o):
    bsz = x.shape[0]
    heads, nope, kvl = w_uk.shape
    kvd = cache.shape[2]
    vh = w_uv.shape[2]
    qkd = nope + kvd - kvl
    xn = rms(x).astype(jnp.bfloat16)
    q = jnp.dot(xn, w_q, preferred_element_type=jnp.float32).astype(jnp.bfloat16).reshape(bsz, heads, qkd)
    kv = jnp.dot(xn, w_dkv, preferred_element_type=jnp.float32)
    kv_new = jnp.concatenate([rms(kv[:, :kvl]), rope(kv[:, kvl:], lens)], axis=-1).astype(jnp.bfloat16)
    q_lat = jnp.einsum('bhd,hdc->bhc', q[:, :, :nope], w_uk, preferred_element_type=jnp.float32).astype(jnp.bfloat16)
    q_rot = rope(q[:, :, nope:].astype(jnp.float32), lens[:, None]).astype(jnp.bfloat16)
    qf = jnp.concatenate([q_lat, q_rot], axis=-1)
    scale = qkd ** -0.5
    s = jnp.einsum('bhc,blc->bhl', qf, cache, preferred_element_type=jnp.float32) * scale
    live = jnp.arange(cache.shape[1])[None, None, :] < lens[:, None, None]
    s = jnp.where(live, s, -jnp.inf)
    s_new = jnp.einsum('bhc,bc->bh', qf, kv_new, preferred_element_type=jnp.float32) * scale
    mx = jnp.maximum(jnp.max(s, axis=2), s_new)
    e = jnp.exp(s - mx[:, :, None])
    e_new = jnp.exp(s_new - mx)
    den = jnp.sum(e, axis=2) + e_new
    p = (e / den[:, :, None]).astype(jnp.bfloat16)
    p_new = (e_new / den).astype(jnp.bfloat16)
    o_all = jnp.einsum('bhl,blc->bhc', p, cache, preferred_element_type=jnp.float32)
    o_lat = (o_all[:, :, :kvl] + p_new.astype(jnp.float32)[:, :, None] * kv_new[:, None, :kvl].astype(jnp.float32)).astype(jnp.bfloat16)
    o = jnp.einsum('bhc,hcv->bhv', o_lat, w_uv, preferred_element_type=jnp.float32).astype(jnp.bfloat16).reshape(bsz, heads * vh)
    a = jnp.dot(o, w_o, preferred_element_type=jnp.float32)
    return (x.astype(jnp.float32) + a).astype(jnp.bfloat16), kv_new


def solution(mesh):
    n = mesh.shape['ep']
    tok_spec = P(('rep', 'ep'))
    row_spec = P(('rep', 'ep'), None)
    cache_spec = P(('rep', 'ep'), None, None)
    exp_spec = P('ep', None, None)

    def local(x, cache, lens, ids, rw, w_q, w_dkv, w_uk, w_uv, w_o, s_gate, s_up, s_down, e_gate, e_up, e_down):
        h1, kv_new = attention(x, cache, lens, w_q, w_dkv, w_uk, w_uv, w_o)
        u = rms(h1).astype(jnp.bfloat16)
        shared = swiglu(u, s_gate, s_up, s_down)
        b_dev, top = ids.shape
        hid = x.shape[1]
        e_loc = e_gate.shape[0]
        n_exp = e_loc * n
        cape = (CAP_FACTOR * b_dev * top + n_exp - 1) // n_exp
        disp, comb = route(ids, rw, n_exp, cape)
        send = jnp.einsum('br,bh->rh', disp, u, preferred_element_type=jnp.float32).astype(jnp.bfloat16)
        recv = lax.all_to_all(send, 'ep', 0, 0, tiled=True)
        xr = recv.reshape(n, e_loc, cape, hid).transpose(1, 0, 2, 3).reshape(e_loc, n * cape, hid)
        g = jnp.einsum('erh,ehi->eri', xr, e_gate, preferred_element_type=jnp.float32)
        v = jnp.einsum('erh,ehi->eri', xr, e_up, preferred_element_type=jnp.float32)
        act = (jax.nn.silu(g) * v).astype(jnp.bfloat16)
        out = jnp.einsum('eri,eih->erh', act, e_down, preferred_element_type=jnp.float32).astype(jnp.bfloat16)
        back = out.reshape(e_loc, n, cape, hid).transpose(1, 0, 2, 3).reshape(n_exp * cape, hid)
        ret = lax.all_to_all(back, 'ep', 0, 0, tiled=True)
        routed = jnp.dot(comb, ret, preferred_element_type=jnp.float32).reshape(-1, b_dev, hid).sum(axis=0)
        y = (h1.astype(jnp.float32) + shared + routed).astype(jnp.bfloat16)
        return y, kv_new

    in_specs = (row_spec, cache_spec, tok_spec, row_spec, row_spec) + (P(),) * 8 + (exp_spec,) * 3
    return jax.shard_map(local, mesh=mesh, in_specs=in_specs, out_specs=(row_spec, row_spec), check_vma=False)
```

profile of v0, /device:TPU:0, one launch (start us, length us, event | category | flops | bytes accessed | tf_op | source)
XLA Modules:
  0.0 311.3 jit_solution(16054211265418728694)
XLA Ops:
  2.3 1.2 fusion.24
  3.5 1.9 fusion.41
  6.9 6.5 %convolution_convert_fusion.1 = bf16[128,3072]{1,0:T(8,128)(2,1)S(1)} fusion(bf16[2048,3072]{1,0:T(8,128)(2,1)} %param.21, bf16[128,2048]{1,0:T(8,128)(2,1)S(1)} %copy-done.2, f32[128]{0:T(128)} %copy-done.8), kind=kOutput, calls=%fused_computation.10 | convolution fusion | flops 1611792384 | bytes 13894144 | tf_op jit(solution)/shard_map/dot_general | solution.py:60
  14.2 2.3 convert_bitcast_fusion.1
  17.0 2.3 multiply_reduce_fusion
  19.4 15.9 %fusion.17 = (f32[128,16]{1,0:T(8,128)S(1)}, f32[128,16,256]{2,1,0:T(8,128)S(1)}) fusion(pred[128,256]{1,0:T(8,128)(4,1)S(1)} %iota_compare_fusion.12, bf16[128,256,576]{1,2,0:T(8,128)(2,1)} %param.17, bf16[128,16,576]{2,0,1:T(8,128)(2,1)} %get-tuple-element.3), kind=kOutput, calls=%fused_computation.30 | convolution fusion | flops 605550592 | bytes 42246144 | tf_op jit(solution)/shard_map/bhc,blc->bhl/dot_general | solution.py:67
  36.8 16.0 %add_convert_fusion = bf16[128,16,512]{2,1,0:T(8,128)(2,1)} fusion(f32[128,512]{1,0:T(8,128)S(1)} %copy-done.6, f32[128,16]{1,0:T(8,128)S(1)} %copy.76, bf16[128,256,576]{1,2,0:T(8,128)(2,1)} %param.17, f32[128,16,256]{2,1,0:T(8,128)S(1)} %get-tuple-element.18, f32[128,16]{1,0:T(8,128)S(1)} %copy.75, f32[128,16]{1,0:T(8,128)S(1)} %copy.73, ...), kind=kOutput, calls=%fused_computation.8 | convolution fusion | flops 542638080 | bytes 38068224 | tf_op jit(solution)/shard_map/bhl,blc->bhc/dot_general | solution.py:77
  52.8 5.0 %fusion.19 = bf16[16,128,128]{1,2,0:T(8,128)(2,1)S(1)} fusion(bf16[16,512,128]{2,1,0:T(8,128)(2,1)} %param.24, bf16[128,16,512]{2,1,0:T(8,128)(2,1)} %add_convert_fusion), kind=kOutput, calls=%fused_computation.36 | convolution fusion | flops 268697600 | bytes 4718592 | tf_op jit(solution)/shard_map/bhc,hcv->bhv/dot_general | solution.py:79
  57.8 4.7 %multiply_reduce_fusion.1 = (f32[128]{0:T(128)S(1)}, f32[128,2048]{1,0:T(8,128)S(1)}) fusion(bf16[128,2048]{0,1:T(8,128)(2,1)S(1)} %bitcast.70, bf16[2048,2048]{1,0:T(8,128)(2,1)} %param.25, bf16[128,2048]{1,0:T(8,128)(2,1)S(1)} %copy-done.3), kind=kOutput, calls=%fused_computation.42 | convolution fusion | flops 1075314560 | bytes 10486272 | tf_op jit(solution)/shard_map/dot_general | solution.py:80
  64.0 1.6 convolution_convert_fusion.2
  66.2 1.9 convolution_convert_fusion
  68.1 75.6 %all_to_all.21 = bf16[8,192,2048]{2,1,0:T(8,128)(2,1)S(1)} all-to-all(bf16[8,192,2048]{2,1,0:T(8,128)(2,1)S(1)} %bitcast.61), channel_id=1, replica_groups=mesh['rep'=1,'ep'=8] {'ep'}, dimensions={0} | all-to-all | bytes 12582912 | tf_op jit(solution)/shard_map/all_to_all | solution.py:102
  143.7 3.3 %copy.85 = bf16[8,8,24,2048]{3,2,0,1:T(8,128)(2,1)} copy(bf16[8,8,24,2048]{3,2,1,0:T(8,128)(2,1)S(1)} %bitcast.63) | data formatting | bytes 12582912 | tf_op jit(solution)/shard_map/reshape | solution.py:103
  146.9 22.2 %fusion.56 = f32[8,192,1408]{2,1,0:T(8,128)} fusion(bf16[8,192,2048]{2,1,0:T(8,128)(2,1)} %bitcast.64, bf16[8,2048,1408]{2,1,0:T(8,128)(2,1)} %param.29), kind=kOutput, calls=%fused_computation.94 | convolution fusion | flops 8858370048 | bytes 61079552 | tf_op jit(solution)/shard_map/erh,ehi->eri/dot_general | solution.py:104
  169.2 25.2 %multiply_convert_fusion.clone.6 = bf16[8,192,1408]{2,1,0:T(8,128)(2,1)} fusion(f32[8,192,1408]{2,1,0:T(8,128)} %fusion.56, bf16[8,192,2048]{2,1,0:T(8,128)(2,1)} %bitcast.65, bf16[8,2048,1408]{2,1,0:T(8,128)(2,1)} %param.30), kind=kOutput, calls=%fused_computation.2.clone.clone.clone.clone.clone.1 | convolution fusion | flops 8871346176 | bytes 65404928 | tf_op jit(solution)/shard_map/erh,ehi->eri/dot_general | solution.py:105
  194.3 18.7 %fusion.3 = bf16[8,192,2048]{2,1,0:T(8,128)(2,1)S(1)} fusion(bf16[8,1408,2048]{2,1,0:T(8,128)(2,1)} %param.31, bf16[8,192,1408]{2,1,0:T(8,128)(2,1)} %multiply_convert_fusion.clone.6), kind=kOutput, calls=%fused_computation.6 | convolution fusion | flops 8861515776 | bytes 56754176 | tf_op jit(solution)/shard_map/eri,eih->erh/dot_general | solution.py:107
  213.0 3.2 %copy.86 = bf16[8,8,24,2048]{3,2,0,1:T(8,128)(2,1)} copy(bf16[8,8,24,2048]{3,2,1,0:T(8,128)(2,1)S(1)} %bitcast.66) | data formatting | bytes 12582912 | tf_op jit(solution)/shard_map/reshape | solution.py:108
  216.2 3.9 %all-to-all-start.1 = ((bf16[8,192,2048]{2,1,0:T(8,128)(2,1)}), bf16[8,192,2048]{2,1,0:T(8,128)(2,1)}, u32[]{:S(2)}, u32[]{:S(2)}) async-start(bf16[8,192,2048]{2,1,0:T(8,128)(2,1)} %bitcast.62), calls=%async_computation.1 | async-start | bytes 12582912 | tf_op jit(solution)/shard_map/all_to_all | solution.py:109
  220.5 3.1 convert_bitcast_fusion
  223.6 2.7 copy.83
  226.3 7.3 %fusion.55 = f32[128,2816]{1,0:T(8,128)} fusion(bf16[2048,2816]{1,0:T(8,128)(2,1)} %param.26, f32[128,2048]{1,0:T(8,128)S(1)} %get-tuple-element.20, f32[128]{0:T(128)S(1)} %add_rsqrt_fusion), kind=kOutput, calls=%fused_computation.93 | convolution fusion | flops 1476919296 | bytes 14025216 | tf_op jit(solution)/shard_map/dot_general | solution.py:28
  233.5 58.1 %all-to-all-done.1 = bf16[8,192,2048]{2,1,0:T(8,128)(2,1)} async-done(((bf16[8,192,2048]{2,1,0:T(8,128)(2,1)}), bf16[8,192,2048]{2,1,0:T(8,128)(2,1)}, u32[]{:S(2)}, u32[]{:S(2)}) %all-to-all-start.1) | async-done | bytes 6291488 | tf_op jit(solution)/shard_map/all_to_all | solution.py:109
  291.6 6.5 %convolution_reduce_fusion = f32[128,2048]{1,0:T(8,128)} fusion(bf16[3,128,1536]{1,2,0:T(8,128)(2,1)S(1)} %bitcast.71, bf16[1536,2048,1]{1,0,2:T(8,128)(2,1)} %bitcast.22), kind=kOutput, calls=%fused_computation.31 | convolution fusion | flops 2416443392 | bytes 8519680 | tf_op jit(solution)/shard_map/dot_general | solution.py:110
  298.1 12.7 %fusion.11 = bf16[128,2048]{1,0:T(8,128)(2,1)} fusion(f32[128,2048]{1,0:T(8,128)} %convolution_reduce_fusion, f32[128,2048]{1,0:T(8,128)S(1)} %get-tuple-element.20, bf16[2816,2048]{1,0:T(8,128)(2,1)} %param.28, bf16[2048,2816]{1,0:T(8,128)(2,1)} %param.27, f32[128,2816]{1,0:T(8,128)} %fusion.55, f32[128]{0:T(128)S(1)} %add_rsqrt_fusion), kind=kOutput, calls=%fused_computation.20 | convolution fusion | flops 2956263424 | bytes 27132416 | tf_op jit(solution)/shard_map/dot_general | solution.py:30
  (59 shorter events, 8.2 us)
Async XLA Ops:
  0.6 2.9 copy-start
  0.6 6.3 %copy-start.2 = (bf16[128,2048]{1,0:T(8,128)(2,1)S(1)}, bf16[128,2048]{1,0:T(8,128)(2,1)}, u32[]{:S(2)}) copy-start(bf16[128,2048]{1,0:T(8,128)(2,1)} %param.16) | copy-start | bytes 1572868
  3.5 2.0 copy-start.8
  6.5 6.9 %copy-start.5 = (bf16[128,576]{0,1:T(8,128)(2,1)}, bf16[128,576]{0,1:T(8,128)(2,1)S(1)}, u32[]{:S(2)}) copy-start(bf16[128,576]{0,1:T(8,128)(2,1)S(1)} %pad_maximum_fusion.1) | copy-start | bytes 442372
  19.4 17.5 %copy-start.6 = (f32[128,512]{1,0:T(8,128)S(1)}, f32[128,512]{1,0:T(8,128)}, u32[]{:S(2)}) copy-start(f32[128,512]{1,0:T(8,128)} %copy.77) | copy-start | bytes 786436
  52.8 5.0 %copy-start.3 = (bf16[128,2048]{1,0:T(8,128)(2,1)S(1)}, bf16[128,2048]{1,0:T(8,128)(2,1)}, u32[]{:S(2)}) copy-start(bf16[128,2048]{1,0:T(8,128)(2,1)} %param.16) | copy-start | bytes 1572868
  57.8 4.8 %copy-start.9 = (s32[128,6]{0,1:T(8,128)S(1)}, s32[128,6]{0,1:T(8,128)}, u32[]{:S(2)}) copy-start(s32[128,6]{0,1:T(8,128)} %param.19) | copy-start | bytes 9220
  63.4 0.6 copy-start.7
  216.2 3.9 %copy-start.10 = (f32[128,6]{0,1:T(8,128)S(1)}, f32[128,6]{0,1:T(8,128)}, u32[]{:S(2)}) copy-start(f32[128,6]{0,1:T(8,128)} %param.20) | copy-start | bytes 9220
  216.2 75.4 %all-to-all-start.1 = ((bf16[8,192,2048]{2,1,0:T(8,128)(2,1)}), bf16[8,192,2048]{2,1,0:T(8,128)(2,1)}, u32[]{:S(2)}, u32[]{:S(2)}) async-start(bf16[8,192,2048]{2,1,0:T(8,128)(2,1)} %bitcast.62), calls=%async_computation.1 | async-start | bytes 12582912 | tf_op jit(solution)/shard_map/all_to_all | solution.py:109
  226.3 65.3 %copy-start.4 = (bf16[3,128,64,24]{1,3,2,0:T(8,128)(2,1)S(1)}, bf16[3,128,64,24]{1,3,2,0:T(8,128)(2,1)}, u32[]{:S(2)}) copy-start(bf16[3,128,64,24]{1,3,2,0:T(8,128)(2,1)} %copy.83) | copy-start | bytes 3538948
  298.1 12.8 %copy-start.1 = (bf16[2048,576]{0,1:T(8,128)(2,1)S(1)}, bf16[2048,576]{0,1:T(8,128)(2,1)}, u32[]{:S(2)}) copy-start(bf16[2048,576]{0,1:T(8,128)(2,1)} %param.22) | copy-start | bytes 7077892
where the time goes:
time: 316 us; the launch traced here: 311 us
  matrix products  152 us (48%)
  blocking collectives  75.6 us (24%)
  waiting for transfers between devices  58.1 us (18%)
  local copies, waits for them, and re-layouts  13.2 us (4%)
  other arithmetic  7.34 us (2%)
  starting transfers between devices  3.86 us (1%)
    all_to_all x1, blocking collectives, local(): recv = lax.all_to_all(send, 'ep', 0, 0, tiled=True)  75.6 us
    all_to_all x1, waiting for transfers between devices, local(): ret = lax.all_to_all(back, 'ep', 0, 0, tiled=True)  58.1 us
    dot_general x1, matrix products, local(): v = jnp.einsum('erh,ehi->eri', xr, e_up, preferred_element_type=jnp.float32)  25.2 us
    dot_general x1, matrix products, local(): jnp.einsum('erh,ehi->eri', xr, e_gate, preferred_element_type=jnp.float32)  22.2 us
    dot_general x1, matrix products, local(): jnp.einsum('eri,eih->erh', act, e_down, preferred_element_type=jnp.float32)  18.7 us
    dot_general x1, matrix products, attention(): jnp.einsum('bhl,blc->bhc', p, cache, preferred_element_type=jnp.float32)  16 us
    dot_general x1, matrix products, attention(): jnp.einsum('bhc,blc->bhl', qf, cache, preferred_element_type=jnp.float32)  15.9 us
    dot_general x1, matrix products, swiglu(): jnp.dot((jax.nn.silu(g) * v).astype(jnp.bfloat16), wd, preferred_element_...  12.7 us
  transfers between devices with their start and end apart: 1, of which 1 were waited for; matrix products, arithmetic and copies ran while one was open for 4% of the time, Pallas kernels for 0%

commit v1 on v0

v1 whole, which is shorter than its diff:
```python
import jax
import jax.numpy as jnp
from jax import lax
from jax.experimental import pallas as pl
from jax.experimental.pallas import tpu as pltpu
from jax.sharding import PartitionSpec as P

EPS = 1e-6
ROPE_BASE = 1.0e4
BF = jnp.bfloat16
F32 = jnp.float32
CAP = 24
CW = 256


def rms(v):
    v = v.astype(jnp.float32)
    return v * lax.rsqrt(jnp.mean(v * v, axis=-1, keepdims=True) + EPS)


def rope(v, pos):
    half = v.shape[-1] // 2
    inv = ROPE_BASE ** (-2.0 * jnp.arange(half, dtype=jnp.float32) / v.shape[-1])
    ang = pos.astype(jnp.float32)[..., None] * inv
    cs = jnp.cos(ang)
    sn = jnp.sin(ang)
    v1 = v[..., :half]
    v2 = v[..., half:]
    return jnp.concatenate([v1 * cs - v2 * sn, v2 * cs + v1 * sn], axis=-1)


def attention(x, cache, lens, w_q, w_dkv, w_uk, w_uv, w_o):
    bsz = x.shape[0]
    heads, nope, kvl = w_uk.shape
    kvd = cache.shape[2]
    vh = w_uv.shape[2]
    qkd = nope + kvd - kvl
    xn = rms(x).astype(jnp.bfloat16)
    q = jnp.dot(xn, w_q, preferred_element_type=jnp.float32).astype(jnp.bfloat16).reshape(bsz, heads, qkd)
    kv = jnp.dot(xn, w_dkv, preferred_element_type=jnp.float32)
    kv_new = jnp.concatenate([rms(kv[:, :kvl]), rope(kv[:, kvl:], lens)], axis=-1).astype(jnp.bfloat16)
    q_lat = jnp.einsum('bhd,hdc->bhc', q[:, :, :nope], w_uk, preferred_element_type=jnp.float32).astype(jnp.bfloat16)
    q_rot = rope(q[:, :, nope:].astype(jnp.float32), lens[:, None]).astype(jnp.bfloat16)
    qf = jnp.concatenate([q_lat, q_rot], axis=-1)
    scale = qkd ** -0.5
    s = jnp.einsum('bhc,blc->bhl', qf, cache, preferred_element_type=jnp.float32) * scale
    live = jnp.arange(cache.shape[1])[None, None, :] < lens[:, None, None]
    s = jnp.where(live, s, -jnp.inf)
    s_new = jnp.einsum('bhc,bc->bh', qf, kv_new, preferred_element_type=jnp.float32) * scale
    mx = jnp.maximum(jnp.max(s, axis=2), s_new)
    e = jnp.exp(s - mx[:, :, None])
    e_new = jnp.exp(s_new - mx)
    den = jnp.sum(e, axis=2) + e_new
    p = (e / den[:, :, None]).astype(jnp.bfloat16)
    p_new = (e_new / den).astype(jnp.bfloat16)
    o_all = jnp.einsum('bhl,blc->bhc', p, cache, preferred_element_type=jnp.float32)
    o_lat = (o_all[:, :, :kvl] + p_new.astype(jnp.float32)[:, :, None] * kv_new[:, None, :kvl].astype(jnp.float32)).astype(jnp.bfloat16)
    o = jnp.einsum('bhc,hcv->bhv', o_lat, w_uv, preferred_element_type=jnp.float32).astype(jnp.bfloat16).reshape(bsz, heads * vh)
    a = jnp.dot(o, w_o, preferred_element_type=jnp.float32)
    return (x.astype(jnp.float32) + a).astype(jnp.bfloat16), kv_new


def moe_kernel(u_ref, h1_ref, wt_ref, sg, su, sd, eg, eu, ed, y_ref,
               u_all, wt_all, rank_s, wsel, pm, cm, xr, act, act_sh, orow, wa, wb, ybase,
               part, rx0, rx1, rx2, rx3, s1, keep0, s2, keep1, s3, keep2,
               sem_a, sem_b, wt_send, wt_recv, g_send, g_recv,
               d_send, d_recv):
    n = 8
    n_loc = 8
    hid = u_ref.shape[1]
    inter = wa.shape[2]
    nc = hid // CW
    me = lax.axis_index('ep')
    core = lax.rem(me, 2)
    chip = me // 2
    cx = lax.rem(chip, 2)
    cy = chip // 2
    sib = chip * 2 + 1 - core
    xn_ = (cy * 2 + 1 - cx) * 2 + core
    yn_ = ((1 - cy) * 2 + cx) * 2 + core
    dg = ((1 - cy) * 2 + 1 - cx) * 2 + core
    dev1 = xn_ * (1 - core) + yn_ * core
    dev2 = yn_ * (1 - core) + xn_ * core

    def load_shared(half):
        cols = pl.ds(half * inter, inter)
        return (pltpu.make_async_copy(sg.at[:, cols], wa.at[2 * half], sem_a.at[2 * half]),
                pltpu.make_async_copy(su.at[:, cols], wa.at[2 * half + 1], sem_a.at[2 * half + 1]))

    def load_expert(e):
        s = lax.rem(e, 2) * 2
        return (pltpu.make_async_copy(eg.at[e], wa.at[s], sem_a.at[s]),
                pltpu.make_async_copy(eu.at[e], wa.at[s + 1], sem_a.at[s + 1]))

    def load_down(c, j):
        cols = pl.ds(pl.multiple_of(c * CW, CW), CW)
        if j < n_loc:
            src = ed.at[j, :, cols]
        else:
            src = sd.at[pl.ds((j - n_loc) * inter, inter), cols]
        return pltpu.make_async_copy(src, wb.at[j], sem_b.at[j])

    def rcopy(src, dst, ssem, rsem, dev):
        return pltpu.make_async_remote_copy(src_ref=src, dst_ref=dst, send_sem=ssem, recv_sem=rsem,
                                            device_id={'ep': dev}, device_id_type=pl.DeviceIdType.MESH)

    for half in range(2):
        for cp in load_shared(half):
            cp.start()

    barrier = pltpu.get_barrier_semaphore()
    for k in range(1, n):
        pl.semaphore_signal(barrier, inc=1, device_id={'ep': lax.rem(me + k, n)}, device_id_type=pl.DeviceIdType.MESH)
    pl.semaphore_wait(barrier, n - 1)

    wt_cp = []
    for k in range(1, n):
        d = lax.rem(me + k, n)
        cp = rcopy(wt_ref.at[pl.ds(pl.multiple_of(d * n_loc, n_loc), n_loc)], wt_all.at[me],
                   wt_send.at[k], wt_recv.at[me], d)
        cp.start()
        wt_cp.append(cp)
    own = [rcopy(u_ref, u_all.at[me], g_send.at[i], g_recv.at[me], d) for i, d in enumerate((dev1, dev2, sib))]
    for cp in own:
        cp.start()
    u_all[me] = u_ref[...]
    wt_all[me] = wt_ref[pl.ds(pl.multiple_of(me * n_loc, n_loc), n_loc), :]

    def glu(lhs, gw, uw):
        g = jnp.dot(lhs, gw, preferred_element_type=F32)
        v = jnp.dot(lhs, uw, preferred_element_type=F32)
        return (g * (1.0 / (1.0 + jnp.exp(-g))) * v).astype(BF)

    cols_n = [(i, min(i + 256, inter)) for i in range(0, inter, 256)]

    for half in range(2):
        for cp in load_shared(half):
            cp.wait()
        for a, b in cols_n:
            act_sh[:, half * inter + a:half * inter + b] = glu(u_ref[...], wa[2 * half, :, a:b], wa[2 * half + 1, :, a:b])
        for cp in load_expert(half):
            cp.start()

    for k in range(1, n):
        s = lax.rem(me + k, n)
        rcopy(wt_all.at[s], wt_all.at[s], wt_send.at[0], wt_recv.at[s], sib).wait_recv()
    w_all = wt_all[...].reshape(n * n_loc, 128)
    ti = lax.broadcasted_iota(jnp.int32, (128, 128), 0)
    tj = lax.broadcasted_iota(jnp.int32, (128, 128), 1)
    tri = (ti < tj).astype(F32).astype(BF)
    hit = w_all > 0.0
    rank = jnp.dot(hit.astype(F32).astype(BF), tri, preferred_element_type=F32)
    rank_s[...] = jnp.where(hit, rank, -1000.0).reshape(n, n_loc, 128)
    row48 = lax.broadcasted_iota(jnp.int32, (2 * CAP, 256), 0).astype(F32)

    def tables(p, carry):
        for e in range(n_loc):
            rk = jnp.concatenate([rank_s[2 * p, e:e + 1, :], rank_s[2 * p + 1, e:e + 1, :] + float(CAP)], axis=1)
            ww = jnp.concatenate([wt_all[2 * p, e:e + 1, :], wt_all[2 * p + 1, e:e + 1, :]], axis=1)
            sel = row48 == rk
            pm[p, e * 2 * CAP:(e + 1) * 2 * CAP, :] = jnp.where(sel, 1.0, 0.0).astype(BF)
            wsel[e * 2 * CAP:(e + 1) * 2 * CAP, :] = jnp.where(sel, ww, 0.0)
        wt = wsel[...].T
        b1 = wt.astype(BF)
        r1 = wt - b1.astype(F32)
        b2 = r1.astype(BF)
        b3 = (r1 - b2.astype(F32)).astype(BF)
        cm[p, 0:256, :] = b1
        cm[p, 256:512, :] = b2
        cm[p, 512:768, :] = b3
        return carry

    lax.fori_loop(0, 4, tables, 0)

    def arrive(s):
        rcopy(u_all.at[s], u_all.at[s], g_send.at[0], g_recv.at[s], sib).wait_recv()

    def partner(s):
        return (s // 2) * 2 + 1 - lax.rem(s, 2)

    def dispatch(p):
        rows = pl.ds(pl.multiple_of(p * 2 * CAP, 16), 2 * CAP)
        for a in range(0, hid, 512):
            uv = u_all[pl.ds(2 * p, 2), :, a:a + 512].reshape(256, 512)
            r = jnp.dot(pm[p], uv, preferred_element_type=F32).astype(BF)
            for e in range(n_loc):
                xr[e, rows, a:a + 512] = r[e * 2 * CAP:(e + 1) * 2 * CAP]

    arrive(sib)
    dispatch(chip)
    arrive(dev1)
    rel = [rcopy(u_all.at[dev1], u_all.at[dev1], g_send.at[3], g_recv.at[dev1], dev2),
           rcopy(u_all.at[dev1], u_all.at[dev1], g_send.at[4], g_recv.at[dev1], sib)]
    rel[0].start()
    rel[1].start()
    arrive(dev2)
    rel.append(rcopy(u_all.at[dev2], u_all.at[dev2], g_send.at[5], g_recv.at[dev2], sib))
    rel[2].start()
    arrive(partner(dev1))
    dispatch(dev1 // 2)
    arrive(partner(dev2))
    dispatch(dev2 // 2)
    arrive(dg)
    rel.append(rcopy(u_all.at[dg], u_all.at[dg], g_send.at[6], g_recv.at[dg], sib))
    rel[3].start()
    arrive(partner(dg))
    dispatch(dg // 2)

    def gate_up(e, carry):
        s = lax.rem(e, 2) * 2
        for cp in load_expert(e):
            cp.wait()
        for a, b in cols_n:
            act[e, :, a:b] = glu(xr[e], wa[s, :, a:b], wa[s + 1, :, a:b])

        @pl.when(e + 2 < n_loc)
        def _():
            for cp in load_expert(e + 2):
                cp.start()

        @pl.when(e == n_loc - 3)
        def _():
            for j in range(n_loc + 2):
                load_down(0, j).start()
        return carry

    lax.fori_loop(0, n_loc, gate_up, 0)

    for cp in own + rel:
        cp.wait_send()
    for cp in wt_cp:
        cp.wait_send()

    def st1(c):
        return rcopy(part.at[lax.rem(c, 2), 1 - core], rx0.at[lax.rem(c, 4)], d_send.at[0, lax.rem(c, 2)], d_recv.at[0, lax.rem(c, 4)], sib)

    def st2(c):
        return rcopy(s1.at[lax.rem(c, 2)], rx1.at[lax.rem(c, 4)], d_send.at[1, lax.rem(c, 2)], d_recv.at[1, lax.rem(c, 4)], dev1)

    def st3(c):
        return rcopy(s2.at[lax.rem(c, 2)], rx2.at[c], d_send.at[2, lax.rem(c, 2)], d_recv.at[2, c], dev2)

    def st4(c):
        return rcopy(s3.at[lax.rem(c, 2)], rx3.at[c], d_send.at[3, lax.rem(c, 2)], d_recv.at[3, c], sib)

    def chunk(c, carry):
        @pl.when(c < nc)
        def _():
            sl = lax.rem(c, 2)
            cols = pl.ds(pl.multiple_of(c * CW, CW), CW)
            for e in range(n_loc):
                load_down(c, e).wait()
                o = jnp.dot(act[e], wb[e], preferred_element_type=F32).astype(BF)
                for p in range(4):
                    orow[p, e * 2 * CAP:(e + 1) * 2 * CAP, :] = o[p * 2 * CAP:(p + 1) * 2 * CAP]

                @pl.when(c + 1 < nc)
                def _():
                    load_down(c + 1, e).start()
            for j in (n_loc, n_loc + 1):
                load_down(c, j).wait()
            sh = (jnp.dot(act_sh[:, :inter], wb[n_loc], preferred_element_type=F32)
                  + jnp.dot(act_sh[:, inter:], wb[n_loc + 1], preferred_element_type=F32))
            ybase[:, cols] = h1_ref[:, cols].astype(F32) + sh

            @pl.when(c + 1 < nc)
            def _():
                for j in (n_loc, n_loc + 1):
                    load_down(c + 1, j).start()
            for dy in (1, 0):
                for dx in (1, 0):
                    py = (1 - cy) if dy else cy
                    px = (1 - cx) if dx else cx
                    p = py * 2 + px
                    r3 = jnp.dot(cm[p], orow[p], preferred_element_type=F32)
                    res = r3[0:256] + r3[256:512] + r3[512:768]
                    for h in range(2):
                        a, b = (dx, dy) if h == 0 else (dy, dx)
                        for cc in range(2):
                            part[sl, h, a, b, cc ^ h] = res[cc * 128:(cc + 1) * 128, h * 128:(h + 1) * 128]
            st1(c).start()

        @pl.when(jnp.logical_and(c >= 1, c < nc + 1))
        def _():
            k = c - 1
            sl = lax.rem(k, 2)
            st1(k).wait_recv()

            @pl.when(k >= 2)
            def _():
                st2(k - 2).wait_send()
            for b in range(2):
                for d in range(2):
                    s1[sl, b, d] = part[sl, core, 1, b, d] + rx0[lax.rem(k, 4), 1, b, d]
            st2(k).start()
            for b in range(2):
                for d in range(2):
                    keep0[sl, b, d] = part[sl, core, 0, b, d] + rx0[lax.rem(k, 4), 0, b, d]
            st1(k).wait_send()

        @pl.when(jnp.logical_and(c >= 2, c < nc + 2))
        def _():
            k = c - 2
            sl = lax.rem(k, 2)
            st2(k).wait_recv()

            @pl.when(k >= 2)
            def _():
                st3(k - 2).wait_send()
            for d in range(2):
                s2[sl, d] = keep0[sl, 1, d] + rx1[lax.rem(k, 4), 1, d]
            st3(k).start()
            for d in range(2):
                keep1[sl, d] = keep0[sl, 0, d] + rx1[lax.rem(k, 4), 0, d]

        @pl.when(jnp.logical_and(c >= 3, c < nc + 3))
        def _():
            k = c - 3
            sl = lax.rem(k, 2)
            st3(k).wait_recv()

            @pl.when(k >= 2)
            def _():
                st4(k - 2).wait_send()
            s3[sl] = keep1[sl, 1] + rx2[k, 1]
            st4(k).start()
            keep2[sl] = keep1[sl, 0] + rx2[k, 0]

        @pl.when(c >= 4)
        def _():
            k = c - 4
            sl = lax.rem(k, 2)
            mine = pl.ds(pl.multiple_of(k * CW + core * 128, 128), 128)
            other = pl.ds(pl.multiple_of(k * CW + (1 - core) * 128, 128), 128)
            st4(k).wait_recv()
            y_ref[:, mine] = (ybase[:, mine] + keep2[sl]).astype(BF)
            y_ref[:, other] = (ybase[:, other] + rx3[k]).astype(BF)
        return carry

    lax.fori_loop(0, nc + 4, chunk, 0)
    for k in (nc - 2, nc - 1):
        st2(k).wait_send()
        st3(k).wait_send()
        st4(k).wait_send()


def moe(u, h1, wt, s_gate, s_up, s_down, e_gate, e_up, e_down):
    t, hid = u.shape
    n_loc, _, inter = e_gate.shape
    nc = hid // CW
    V = pltpu.VMEM
    D = pltpu.SemaphoreType.DMA
    vm = pl.BlockSpec(memory_space=pltpu.VMEM)
    an = pl.BlockSpec(memory_space=pl.ANY)
    return pl.pallas_call(
        moe_kernel,
        out_shape=jax.ShapeDtypeStruct((t, hid), BF),
        in_specs=[vm] * 3 + [an] * 6,
        out_specs=vm,
        scratch_shapes=[
            V((8, t, hid), BF), V((8, n_loc, t), F32), V((8, n_loc, t), F32), V((n_loc * 2 * CAP, 256), F32),
            V((4, n_loc * 2 * CAP, 256), BF), V((4, 768, n_loc * 2 * CAP), BF),
            V((n_loc, 8 * CAP, hid), BF), V((n_loc, 8 * CAP, inter), BF), V((t, 2 * inter), BF),
            V((4, n_loc * 2 * CAP, CW), BF),
            V((4, hid, inter), BF), V((n_loc + 2, inter, CW), BF), V((t, hid), F32),
            V((2, 2, 2, 2, 2, t, 128), F32), V((4, 2, 2, 2, t, 128), F32), V((4, 2, 2, t, 128), F32),
            V((nc, 2, t, 128), F32), V((nc, t, 128), F32),
            V((2, 2, 2, t, 128), F32), V((2, 2, 2, t, 128), F32),
            V((2, 2, t, 128), F32), V((2, 2, t, 128), F32), V((2, t, 128), F32), V((2, t, 128), F32),
            D((4,)), D((n_loc + 2,)), D((8,)), D((8,)), D((7,)), D((8,)),
            D((4, 2)), D((4, nc)),
        ],
        compiler_params=pltpu.CompilerParams(collective_id=0, has_side_effects=True, vmem_limit_bytes=67043328),
        name='moe',
    )(u, h1, wt, s_gate, s_up, s_down, e_gate, e_up, e_down)


def solution(mesh):
    tok_spec = P(('rep', 'ep'))
    row_spec = P(('rep', 'ep'), None)
    cache_spec = P(('rep', 'ep'), None, None)
    exp_spec = P('ep', None, None)

    def local(x, cache, lens, ids, rw, w_q, w_dkv, w_uk, w_uv, w_o, s_gate, s_up, s_down, e_gate, e_up, e_down):
        n_exp = e_gate.shape[0] * mesh.shape['ep']
        wt = jnp.sum(jnp.where(ids.T[:, None, :] == jnp.arange(n_exp)[None, :, None], rw.T[:, None, :], 0.0), axis=0)
        h1, kv_new = attention(x, cache, lens, w_q, w_dkv, w_uk, w_uv, w_o)
        u = rms(h1).astype(jnp.bfloat16)
        y = moe(u, h1, wt, s_gate, s_up, s_down, e_gate, e_up, e_down)
        return y, kv_new

    in_specs = (row_spec, cache_spec, tok_spec, row_spec, row_spec) + (P(),) * 8 + (exp_spec,) * 3
    return jax.shard_map(local, mesh=mesh, in_specs=in_specs, out_specs=(row_spec, row_spec), check_vma=False)
```

time: 316 us -> 188 us (0.59); the launches traced: 311 us -> 187 us
  Pallas kernels: 0 us -> 116 us
  matrix products: 152 us -> 55.2 us
  blocking collectives: 75.6 us -> 0 us
  waiting for transfers between devices: 58.1 us -> 0 us
  local copies, waits for them, and re-layouts: 13.2 us -> 6.29 us
  starting transfers between devices: 3.86 us -> 0 us
    pallas_call x0 -> x1, Pallas kernels: none -> 116 us  [moe(): pl.pallas_call(moe_kernel, out_shape=jax.ShapeDtypeStruct((t, hid), BF),...]
    dot_general x10 -> x1, matrix products: 99.5 us -> 2.69 us  [attention(): jnp.einsum('bhc,bc->bh', qf, kv_new, preferred_element_type=jnp.float32)]
    all_to_all x1 -> x0, blocking collectives: 75.6 us -> none  [local(): recv = lax.all_to_all(send, 'ep', 0, 0, tiled=True)]
    all_to_all x1 -> x0, waiting for transfers between devices: 58.1 us -> none  [local(): ret = lax.all_to_all(back, 'ep', 0, 0, tiled=True)]
    reshape x2 -> x0, local copies, waits for them, and re-layouts: 6.5 us -> none  [the longest x1 3.27 us: local(): recv.reshape(n, e_loc, cape, hid).transpose(1, 0, 2, 3)]
    all_to_all x1 -> x0, starting transfers between devices: 3.86 us -> none  [local(): ret = lax.all_to_all(back, 'ep', 0, 0, tiled=True)]
    convert_element_type x4 -> x0, local copies, waits for them, and re-layouts: 3.47 us -> none  [the longest x1 2.66 us: route(): jnp.einsum('jbke,bkr->jber', hw, at, preferred_element_type=jnp.float32)]
    unnamed x25 -> x24, local copies, waits for them, and re-layouts: 1.22 us -> 4.66 us
  transfers between devices with their start and end apart: 1 -> 0, of which waited for: 1 -> 0; matrix products, arithmetic and copies ran while one was open for 4% -> 0% of each run, Pallas kernels for 0% -> 0%
where the time goes in v1:
time: 188 us; the launch traced here: 187 us
  Pallas kernels  116 us (62%)
  matrix products  55.2 us (29%)
  other arithmetic  8.56 us (5%)
  local copies, waits for them, and re-layouts  6.29 us (3%)
    pallas_call x1, Pallas kernels, moe(): pl.pallas_call(moe_kernel, out_shape=jax.ShapeDtypeStruct((t, hid), BF),...  116 us
    dot_general x1, matrix products, attention(): jnp.einsum('bhc,blc->bhl', qf, cache, preferred_element_type=jnp.float32)  16.9 us
    dot_general x1, matrix products, attention(): jnp.einsum('bhl,blc->bhc', p, cache, preferred_element_type=jnp.float32)  16 us
    dot_general x1, matrix products, attention(): jnp.dot(xn, w_q, preferred_element_type=jnp.float32).astype(jnp.bfloat16)  6.49 us
    dot_general x1, matrix products, attention(): jnp.einsum('bhc,hcv->bhv', o_lat, w_uv, preferred_element_type=jnp.float32)  4.9 us
    dot_general x1, matrix products, attention(): a = jnp.dot(o, w_o, preferred_element_type=jnp.float32)  4.77 us
    unnamed x24, local copies, waits for them, and re-layouts  4.66 us

profile of v1, /device:TPU:0, one launch (start us, length us, event | category | flops | bytes accessed | tf_op | source)
XLA Modules:
  0.0 187.2 jit_solution(2510296249773732420)
XLA Ops:
  0.7 1.3 fusion.18
  2.0 2.7 %fusion.26 = f32[128,576]{0,1:T(8,128)S(1)} fusion(bf16[2048,576]{0,1:T(8,128)(2,1)} %param.22, bf16[128,2048]{1,0:T(8,128)(2,1)} %param.16, f32[128]{0:T(128)S(1)} %add_rsqrt_fusion.2), kind=kOutput, calls=%fused_computation.38 | convolution fusion | flops 302776320 | bytes 3179008 | tf_op jit(solution)/shard_map/dot_general | solution.py:40
  4.7 0.1 multiply_cosine_fusion
  5.1 6.5 %convolution_convert_fusion = bf16[128,3072]{1,0:T(8,128)(2,1)S(1)} fusion(bf16[2048,3072]{1,0:T(8,128)(2,1)} %param.21, bf16[128,2048]{1,0:T(8,128)(2,1)S(1)} %copy-done, f32[128]{0:T(128)S(1)} %add_rsqrt_fusion.2), kind=kOutput, calls=%fused_computation.3 | convolution fusion | flops 1611792384 | bytes 13894144 | tf_op jit(solution)/shard_map/dot_general | solution.py:39
  11.6 0.4 copy.35
  12.0 0.3 copy.48
  12.4 0.5 subtract_convert_fusion
  12.8 1.0 copy-done.5
  13.9 0.8 convert_bitcast_fusion
  14.6 0.5 pad_maximum_fusion
  15.3 0.6 copy-done.3
  15.9 0.9 copy.44
  16.9 2.7 %fusion.3 = f32[128,1,16]{2,1,0:T(1,128)S(1)} fusion(bf16[128,576,1]{1,2,0:T(2,128)(2,1)} %copy.44, bf16[128,16,576]{2,0,1:T(8,128)(2,1)S(1)} %pad_maximum_fusion), kind=kOutput, calls=%fused_computation.7 | convolution fusion | flops 2359296 | bytes 2514944 | tf_op jit(solution)/shard_map/bhc,bc->bh/dot_general | solution.py:49
  19.6 16.9 %fusion.11 = (f32[128,16]{1,0:T(8,128)S(1)}, f32[128,16,256]{2,1,0:T(8,128)}) fusion(pred[128,256]{1,0:T(8,128)(4,1)S(1)} %iota_compare_fusion.1, bf16[128,256,576]{1,2,0:T(8,128)(2,1)} %param.17, bf16[128,16,576]{2,0,1:T(8,128)(2,1)S(1)} %pad_maximum_fusion), kind=kOutput, calls=%fused_computation.17 | convolution fusion | flops 605550592 | bytes 42246144 | tf_op jit(solution)/shard_map/bhc,blc->bhl/dot_general | solution.py:46
  36.5 2.6 %fusion.12 = f32[128,16]{1,0:T(8,128)S(1)} fusion(f32[128,16,256]{2,1,0:T(8,128)} %get-tuple-element.13, f32[128,16]{1,0:T(8,128)S(1)} %multiply_maximum_fusion, pred[128,256]{1,0:T(8,128)(4,1)S(1)} %iota_compare_fusion.1), kind=kLoop, calls=%fused_computation.18 | loop fusion | flops 2095104 | bytes 2146304 | tf_op jit(solution)/shard_map/reduce_sum | solution.py:53
  39.3 16.0 %add_convert_fusion = bf16[128,16,512]{2,1,0:T(8,128)(2,1)} fusion(f32[128,512]{1,0:T(8,128)S(1)} %copy.41, f32[128,16]{1,0:T(8,128)S(1)} %get-tuple-element.7, bf16[128,256,576]{1,2,0:T(8,128)(2,1)} %param.17, f32[128,16,256]{2,1,0:T(8,128)S(1)} %copy-done.1, f32[128,16]{1,0:T(8,128)S(1)} %get-tuple-element.6, f32[128,16]{1,0:T(8,128)S(1)} %multiply_maximum_fusion, ...), kind=kOutput, calls=%fused_computation.2 | convolution fusion | flops 542638080 | bytes 38068224 | tf_op jit(solution)/shard_map/bhl,blc->bhc/dot_general | solution.py:56
  55.3 4.9 %fusion.13 = bf16[16,128,128]{1,2,0:T(8,128)(2,1)S(1)} fusion(bf16[16,512,128]{2,1,0:T(8,128)(2,1)} %param.24, bf16[128,16,512]{2,1,0:T(8,128)(2,1)} %add_convert_fusion), kind=kOutput, calls=%fused_computation.23 | convolution fusion | flops 268697600 | bytes 4718592 | tf_op jit(solution)/shard_map/bhc,hcv->bhv/dot_general | solution.py:58
  60.2 4.8 %fusion.16 = (f32[128]{0:T(128)S(1)}, bf16[128,2048]{1,0:T(8,128)(2,1)S(1)}) fusion(bf16[128,2048]{0,1:T(8,128)(2,1)S(1)} %bitcast.22, bf16[2048,2048]{1,0:T(8,128)(2,1)} %param.25, bf16[128,2048]{1,0:T(8,128)(2,1)S(1)} %copy-done), kind=kOutput, calls=%fused_computation.24 | convolution fusion | flops 1075314560 | bytes 9961984 | tf_op jit(solution)/shard_map/dot_general | solution.py:59
  65.0 0.8 copy-done.2
  65.8 0.9 fusion.17.u_ref
  66.8 0.6 select_reduce_fusion.wt_ref
  67.4 116.3 %moe.1 = bf16[128,2048]{1,0:T(8,128)(2,1)} custom-call(bf16[128,2048]{1,0:T(8,128)(2,1)} %fusion.17.u_ref, bf16[128,2048]{1,0:T(8,128)(2,1)} %copy-done.2, f32[64,128]{1,0:T(8,128)} %select_reduce_fusion.wt_ref, bf16[2048,2816]{1,0:T(8,128)(2,1)} %sg.1, bf16[2048,2816]{1,0:T(8,128)(2,1)} %su.1, bf16[2816,2048]{1,0:T(8,128)(2,1)} %sd.1, ...), custom_call_target="tpu_custom_call" | custom-call | tf_op jit(solution)/shard_map/moe/pallas_call | solution.py:355
  183.7 1.6 pad_maximum_fusion.1
  185.3 1.9 %copy.60 = bf16[128,2048]{1,0:T(8,128)(2,1)} copy(bf16[128,2048]{1,0:T(8,128)(2,1)} %moe.1) | data formatting | bytes 1048576
  (35 shorter events, 0.8 us)
Async XLA Ops:
  0.6 4.4 %copy-start = (bf16[128,2048]{1,0:T(8,128)(2,1)S(1)}, bf16[128,2048]{1,0:T(8,128)(2,1)}, u32[]{:S(2)}) copy-start(bf16[128,2048]{1,0:T(8,128)(2,1)} %param.16) | copy-start | bytes 1572868
  0.6 4.0 %copy-start.10 = (s32[128]{0:T(128)S(1)}, s32[128]{0:T(128)}, u32[]{:S(2)}) copy-start(s32[128]{0:T(128)} %param.18) | copy-start | bytes 1540
  4.8 10.4 %copy-start.6 = (bf16[128,32]{0,1:T(8,128)(2,1)}, bf16[128,32]{0,1:T(8,128)(2,1)S(1)}, u32[]{:S(2)}) copy-start(bf16[128,32]{0,1:T(8,128)(2,1)S(1)} %get-tuple-element.10) | copy-start | bytes 24580
  4.9 10.4 %copy-start.7 = (bf16[128,32]{0,1:T(8,128)(2,1)}, bf16[128,32]{0,1:T(8,128)(2,1)S(1)}, u32[]{:S(2)}) copy-start(bf16[128,32]{0,1:T(8,128)(2,1)S(1)} %get-tuple-element.11) | copy-start | bytes 24580
  12.3 1.6 copy-start.5
  15.3 0.7 copy-start.3
  36.5 2.7 %copy-start.4 = (bf16[128,512]{0,1:T(8,128)(2,1)S(1)}, bf16[128,512]{0,1:T(8,128)(2,1)}, u32[]{:S(2)}) copy-start(bf16[128,512]{0,1:T(8,128)(2,1)} %copy-done.3) | copy-start | bytes 393220
  36.5 2.8 %copy-start.1 = (f32[128,16,256]{2,1,0:T(8,128)S(1)}, f32[128,16,256]{2,1,0:T(8,128)}, u32[]{:S(2)}) copy-start(f32[128,16,256]{2,1,0:T(8,128)} %get-tuple-element.13) | copy-start | bytes 6291460
  60.2 6.6 %copy-start.8 = (f32[128,6]{0,1:T(8,128)S(1)}, f32[128,6]{0,1:T(8,128)}, u32[]{:S(2)}) copy-start(f32[128,6]{0,1:T(8,128)} %param.20) | copy-start | bytes 9220
  60.2 6.6 %copy-start.9 = (s32[128,6]{0,1:T(8,128)S(1)}, s32[128,6]{0,1:T(8,128)}, u32[]{:S(2)}) copy-start(s32[128,6]{0,1:T(8,128)} %param.19) | copy-start | bytes 9220
  65.0 0.8 copy-start.2

commit v2 on v1

v2 whole, which is shorter than its diff:
```python
import jax
import jax.numpy as jnp
from jax import lax
from jax.experimental import pallas as pl
from jax.experimental.pallas import tpu as pltpu
from jax.sharding import PartitionSpec as P

EPS = 1e-6
ROPE_BASE = 1.0e4
BF = jnp.bfloat16
F32 = jnp.float32
CAP = 24
CW = 256
NA = 768
NSUB = 4


NB = 16
RING = 3


def attn_kernel(lens_ref, ids_ref, rw_ref, x_ref, cs_ref, sn_ref, wq_h, wdkv_h, wuk_h, wuv_h, wo_h, cache_h,
                h1_ref, u_ref, kvn_ref, wt_ref,
                wq, wdkv, wuk, wuv, wo, cbuf, qs, kvs, os, oc,
                sem_w, sem_q, sem_c):
    t, hid = x_ref.shape
    heads, nope, kvl = wuk.shape
    kvd = cbuf.shape[2]
    rot = kvd - kvl
    qkd = nope + rot
    length = cbuf.shape[3]
    vh = wuv.shape[2]
    nblk = t // NB
    qw = 4 * qkd
    nq = heads // 4
    scale = qkd ** -0.5

    cp_dkv = pltpu.make_async_copy(wdkv_h, wdkv, sem_w.at[0])
    cp_uk = pltpu.make_async_copy(wuk_h, wuk, sem_w.at[1])
    cp_uv = pltpu.make_async_copy(wuv_h, wuv, sem_w.at[2])
    cp_o = pltpu.make_async_copy(wo_h, wo, sem_w.at[3])
    cp_q = [pltpu.make_async_copy(wq_h.at[:, i * qw:(i + 1) * qw], wq.at[i], sem_q.at[i]) for i in range(nq)]

    def load(b):
        sl = lax.rem(b, RING)
        return pltpu.make_async_copy(cache_h.at[pl.ds(b * NB, NB)], cbuf.at[sl], sem_c.at[sl])

    cp_dkv.start()
    cp_q[0].start()
    cp_uk.start()
    for cp in cp_q[1:]:
        cp.start()
    for b in range(RING):
        load(b).start()
    cp_uv.start()
    cp_o.start()

    cs = cs_ref[...]
    sn = sn_ref[...]
    lane = lax.broadcasted_iota(jnp.int32, (t, 128), 1)
    low = lax.rem(lane, rot) < rot // 2

    def rope2(v):
        sw = jnp.where(low, pltpu.roll(v, 128 - rot // 2, 1), pltpu.roll(v, rot // 2, 1))
        return v * cs + sw * sn

    xf = x_ref[...].astype(F32)
    xn = (xf * lax.rsqrt(jnp.mean(xf * xf, axis=-1, keepdims=True) + EPS)).astype(BF)

    ex = lax.broadcasted_iota(jnp.int32, wt_ref.shape, 0)
    wt = jnp.zeros(wt_ref.shape, F32)
    for k in range(ids_ref.shape[0]):
        wt = wt + jnp.where(ids_ref[k:k + 1, :] == ex, rw_ref[k:k + 1, :], 0.0)
    wt_ref[...] = wt

    cp_dkv.wait()
    kv = lax.dot_general(xn, wdkv[...], (((1,), (1,)), ((), ())), preferred_element_type=F32)
    kl = kv[:, 0:kvl]
    kl = (kl * lax.rsqrt(jnp.mean(kl * kl, axis=-1, keepdims=True) + EPS)).astype(BF)
    kr = kv[:, kvl:kvd]
    kr = rope2(jnp.concatenate([kr, kr], axis=1)).astype(BF)
    kvs[:, 0:kvl] = kl.astype(F32)
    kvs[:, kvl:kvl + 128] = jnp.where(lane < rot, kr.astype(F32), 0.0)
    kvn_ref[...] = kvs[...].T[0:kvd].astype(BF)

    for i in range(nq):
        cp_q[i].wait()
        qc = jnp.dot(xn, wq[i], preferred_element_type=F32).astype(BF).astype(F32)
        if i == 0:
            cp_uk.wait()
        for j in range(2):
            o0 = j * 2 * qkd
            h = i * 4 + j * 2
            n0 = qc[:, o0:o0 + nope].astype(BF)
            n1 = qc[:, o0 + qkd:o0 + qkd + nope].astype(BF)
            r = jnp.concatenate([qc[:, o0 + nope:o0 + qkd], qc[:, o0 + qkd + nope:o0 + 2 * qkd]], axis=1)
            r = rope2(r).astype(BF).astype(F32)
            qs[:, h, 0:kvl] = jnp.dot(n0, wuk[h], preferred_element_type=F32).astype(BF).astype(F32)
            qs[:, h + 1, 0:kvl] = jnp.dot(n1, wuk[h + 1], preferred_element_type=F32).astype(BF).astype(F32)
            qs[:, h, kvl:kvl + 128] = jnp.where(lane < rot, r, 0.0)
            qs[:, h + 1, kvl:kvl + 128] = jnp.where(lane < rot, pltpu.roll(r, rot, 1), 0.0)

    pos = lax.broadcasted_iota(jnp.int32, (heads, length), 1)

    def block(b, carry):
        sl = lax.rem(b, RING)
        load(b).wait()
        ss = []
        sns = []
        for i in range(NB):
            qf = qs[b * NB + i]
            qb = qf[:, 0:kvd].astype(BF)
            ss.append(jnp.dot(qb, cbuf[sl, i], preferred_element_type=F32))
            sns.append(jnp.sum(qf * kvs[pl.ds(b * NB + i, 1), :], axis=1, keepdims=True) * scale)
        for i in range(NB):
            s = jnp.where(pos < lens_ref[b * NB + i], ss[i] * scale, -jnp.inf)
            mx = jnp.maximum(jnp.max(s, axis=1, keepdims=True), sns[i])
            e = jnp.exp(s - mx)
            en = jnp.exp(sns[i] - mx)
            den = jnp.sum(e, axis=1, keepdims=True) + en
            p = (e / den).astype(BF)
            pn = (en / den).astype(BF).astype(F32)
            o = lax.dot_general(p, cbuf[sl, i, 0:kvl, :], (((1,), (1,)), ((), ())), preferred_element_type=F32)
            os[:, b * NB + i, :] = o + pn * kvs[pl.ds(b * NB + i, 1), 0:kvl]

        @pl.when(b + RING < nblk)
        def _():
            load(b + RING).start()
        return carry

    lax.fori_loop(0, nblk, block, 0)

    cp_uv.wait()
    for h in range(heads):
        oc[:, h * vh:(h + 1) * vh] = jnp.dot(os[h].astype(BF), wuv[h], preferred_element_type=F32).astype(BF)
    cp_o.wait()
    ssq = jnp.zeros((t, 1), F32)
    for a in range(0, hid, 512):
        h1 = (x_ref[:, a:a + 512].astype(F32)
              + jnp.dot(oc[...], wo[:, a:a + 512], preferred_element_type=F32)).astype(BF)
        h1_ref[:, a:a + 512] = h1
        hf = h1.astype(F32)
        ssq = ssq + jnp.sum(hf * hf, axis=1, keepdims=True)
    inv = lax.rsqrt(ssq * (1.0 / hid) + EPS)
    u_ref[...] = (h1_ref[...].astype(F32) * inv).astype(BF)


def attention(x, cache, lens, ids, rw, n_exp, w_q, w_dkv, w_uk, w_uv, w_o):
    t, hid = x.shape
    heads, nope, kvl = w_uk.shape
    _, length, kvd = cache.shape
    vh = w_uv.shape[2]
    rot = kvd - kvl
    half = rot // 2
    lane = jnp.arange(128)
    ang = lens.astype(F32)[:, None] * (ROPE_BASE ** (-2.0 * (lane % half).astype(F32) / rot))[None, :]
    cs4 = jnp.cos(ang)
    sn4 = jnp.sin(ang) * jnp.where(lane % rot < half, -1.0, 1.0)[None, :]
    V = pltpu.VMEM
    D = pltpu.SemaphoreType.DMA
    vm = pl.BlockSpec(memory_space=pltpu.VMEM)
    an = pl.BlockSpec(memory_space=pl.ANY)
    h1, u, kvt, wt = pl.pallas_call(
        attn_kernel,
        out_shape=(jax.ShapeDtypeStruct((t, hid), BF), jax.ShapeDtypeStruct((t, hid), BF),
                   jax.ShapeDtypeStruct((kvd, t), BF), jax.ShapeDtypeStruct((n_exp, t), F32)),
        in_specs=[pl.BlockSpec(memory_space=pltpu.SMEM)] + [vm] * 5 + [an] * 6,
        out_specs=(vm, vm, vm, vm),
        scratch_shapes=[
            V((heads // 4, hid, 4 * (nope + rot)), BF), V((kvd, hid), BF), V((heads, nope, kvl), BF),
            V((heads, kvl, vh), BF), V((heads * vh, hid), BF), V((RING, NB, kvd, length), BF),
            V((t, heads, kvl + 128), F32), V((t, kvl + 128), F32), V((heads, t, kvl), F32), V((t, heads * vh), BF),
            D((4,)), D((heads // 4,)), D((RING,)),
        ],
        compiler_params=pltpu.CompilerParams(vmem_limit_bytes=67043328),
        name='attn',
    )(lens, ids.T, rw.T, x, cs4, sn4, w_q, w_dkv.T, w_uk, w_uv, w_o, cache.transpose(0, 2, 1))
    return h1, u, kvt.T, wt


def moe_kernel(u_ref, h1_ref, wt_ref, sg, su, sd, eg, eu, ed, y_ref,
               u_all, wt_all, rank_s, wsel, pm, cm, xr, act, act_sh, orow, wa, wc, wb, ybase,
               part, rx0, rx1, rx2, rx3, s1, keep0, s2, keep1, s3, keep2,
               sem_a, sem_b, wt_send, wt_recv, g_send, g_recv,
               d_send, d_recv):
    n = 8
    n_loc = 8
    hid = u_ref.shape[1]
    inter = act.shape[2]
    na = wa.shape[3]
    nc = hid // CW
    me = lax.axis_index('ep')
    core = lax.rem(me, 2)
    chip = me // 2
    cx = lax.rem(chip, 2)
    cy = chip // 2
    sib = chip * 2 + 1 - core
    xn_ = (cy * 2 + 1 - cx) * 2 + core
    yn_ = ((1 - cy) * 2 + cx) * 2 + core
    dg = ((1 - cy) * 2 + 1 - cx) * 2 + core
    dev1 = xn_ * (1 - core) + yn_ * core
    dev2 = yn_ * (1 - core) + xn_ * core

    def load_unit(srcs, base, slot, part_):
        buf, width, off = (wa, na, 0) if part_ == 0 else (wc, inter - na, na)
        return [pltpu.make_async_copy(src.at[:, pl.ds(base + off, width)], buf.at[slot, i], sem_a.at[part_, slot, i])
                for i, src in enumerate(srcs)]

    def load_shared(half, part_):
        return load_unit((sg, su), half * inter, half, part_)

    def load_expert(e, part_):
        return load_unit((eg.at[e], eu.at[e]), 0, lax.rem(e, 2), part_)

    def load_down(c, j):
        cols = pl.ds(pl.multiple_of(c * CW, CW), CW)
        if j < n_loc:
            src = ed.at[j, :, cols]
        else:
            src = sd.at[pl.ds((j - n_loc) * inter, inter), cols]
        return pltpu.make_async_copy(src, wb.at[j], sem_b.at[j])

    def rcopy(src, dst, ssem, rsem, dev):
        return pltpu.make_async_remote_copy(src_ref=src, dst_ref=dst, send_sem=ssem, recv_sem=rsem,
                                            device_id={'ep': dev}, device_id_type=pl.DeviceIdType.MESH)

    for half in range(2):
        for part_ in range(2):
            for cp in load_shared(half, part_):
                cp.start()

    barrier = pltpu.get_barrier_semaphore()
    for k in range(1, n):
        pl.semaphore_signal(barrier, inc=1, device_id={'ep': lax.rem(me + k, n)}, device_id_type=pl.DeviceIdType.MESH)
    pl.semaphore_wait(barrier, n - 1)

    wt_cp = []
    for k in range(1, n):
        d = lax.rem(me + k, n)
        cp = rcopy(wt_ref.at[pl.ds(pl.multiple_of(d * n_loc, n_loc), n_loc)], wt_all.at[me],
                   wt_send.at[k], wt_recv.at[me], d)
        cp.start()
        wt_cp.append(cp)
    rsub = u_ref.shape[0] // NSUB

    def ucopy(kind, s, i, dev, src=None):
        rows = pl.ds(i * rsub, rsub)
        return rcopy(u_all.at[s, rows] if src is None else src.at[rows], u_all.at[s, rows],
                     g_send.at[kind, i], g_recv.at[s, i], dev)

    own = [ucopy(kind, me, i, d, u_ref) for i in range(NSUB) for kind, d in enumerate((dev1, dev2, sib))]
    for cp in own:
        cp.start()
    u_all[me] = u_ref[...]
    wt_all[me] = wt_ref[pl.ds(pl.multiple_of(me * n_loc, n_loc), n_loc), :]

    def glu(lhs, gw, uw):
        g = jnp.dot(lhs, gw, preferred_element_type=F32)
        v = jnp.dot(lhs, uw, preferred_element_type=F32)
        return (g * (1.0 / (1.0 + jnp.exp(-g))) * v).astype(BF)

    def glu_unit(lhs, slot, part_, store):
        buf, width, off = (wa, na, 0) if part_ == 0 else (wc, inter - na, na)
        for a in range(0, width, 256):
            b = min(a + 256, width)
            store(off + a, off + b, glu(lhs, buf[slot, 0, :, a:b], buf[slot, 1, :, a:b]))

    for half in range(2):
        for part_ in range(2):
            for cp in load_shared(half, part_):
                cp.wait()

            def put(a, b, v):
                act_sh[:, half * inter + a:half * inter + b] = v

            glu_unit(u_ref[...], half, part_, put)
            for cp in load_expert(half, part_):
                cp.start()

    for k in range(1, n):
        s = lax.rem(me + k, n)
        rcopy(wt_all.at[s], wt_all.at[s], wt_send.at[0], wt_recv.at[s], sib).wait_recv()
    w_all = wt_all[...].reshape(n * n_loc, 128)
    ti = lax.broadcasted_iota(jnp.int32, (128, 128), 0)
    tj = lax.broadcasted_iota(jnp.int32, (128, 128), 1)
    tri = (ti < tj).astype(F32).astype(BF)
    hit = w_all > 0.0
    rank = jnp.dot(hit.astype(F32).astype(BF), tri, preferred_element_type=F32)
    rank_s[...] = jnp.where(hit, rank, -1000.0).reshape(n, n_loc, 128)
    row48 = lax.broadcasted_iota(jnp.int32, (2 * CAP, 256), 0).astype(F32)

    def tables(p, carry):
        for e in range(n_loc):
            rk = jnp.concatenate([rank_s[2 * p, e:e + 1, :], rank_s[2 * p + 1, e:e + 1, :] + float(CAP)], axis=1)
            ww = jnp.concatenate([wt_all[2 * p, e:e + 1, :], wt_all[2 * p + 1, e:e + 1, :]], axis=1)
            sel = row48 == rk
            pm[p, e * 2 * CAP:(e + 1) * 2 * CAP, :] = jnp.where(sel, 1.0, 0.0).astype(BF)
            wsel[e * 2 * CAP:(e + 1) * 2 * CAP, :] = jnp.where(sel, ww, 0.0)
        wt = wsel[...].T
        b1 = wt.astype(BF)
        r1 = wt - b1.astype(F32)
        b2 = r1.astype(BF)
        b3 = (r1 - b2.astype(F32)).astype(BF)
        cm[p, 0:256, :] = b1
        cm[p, 256:512, :] = b2
        cm[p, 512:768, :] = b3
        return carry

    lax.fori_loop(0, 4, tables, 0)

    def arrive(s, subs=range(NSUB)):
        for i in subs:
            ucopy(0, s, i, sib).wait_recv()

    def partner(s):
        return (s // 2) * 2 + 1 - lax.rem(s, 2)

    def dispatch(p):
        rows = pl.ds(pl.multiple_of(p * 2 * CAP, 16), 2 * CAP)
        for a in range(0, hid, 512):
            uv = u_all[pl.ds(2 * p, 2), :, a:a + 512].reshape(256, 512)
            r = jnp.dot(pm[p], uv, preferred_element_type=F32).astype(BF)
            for e in range(n_loc):
                xr[e, rows, a:a + 512] = r[e * 2 * CAP:(e + 1) * 2 * CAP]

    rel = []

    def relay(kinds, s, devs, i):
        arrive(s, (i,))
        for kind, dev in zip(kinds, devs):
            cp = ucopy(kind, s, i, dev)
            cp.start()
            rel.append(cp)

    arrive(sib)
    dispatch(chip)
    for i in range(NSUB):
        relay((3, 4), dev1, (dev2, sib), i)
        relay((5,), dev2, (sib,), i)
    arrive(partner(dev1))
    dispatch(dev1 // 2)
    arrive(partner(dev2))
    dispatch(dev2 // 2)
    for i in range(NSUB):
        relay((6,), dg, (sib,), i)
    arrive(partner(dg))
    dispatch(dg // 2)

    def gate_up(e, carry):
        def put(a, b, v):
            act[e, :, a:b] = v

        for part_ in range(2):
            for cp in load_expert(e, part_):
                cp.wait()
            glu_unit(xr[e], lax.rem(e, 2), part_, put)

            @pl.when(e + 2 < n_loc)
            def _():
                for cp in load_expert(e + 2, part_):
                    cp.start()

        @pl.when(e == n_loc - 3)
        def _():
            for j in range(n_loc + 2):
                load_down(0, j).start()
        return carry

    lax.fori_loop(0, n_loc, gate_up, 0)

    for cp in own + rel:
        cp.wait_send()
    for cp in wt_cp:
        cp.wait_send()

    def st1(c):
        return rcopy(part.at[lax.rem(c, 2), 1 - core], rx0.at[lax.rem(c, 4)], d_send.at[0, lax.rem(c, 2)], d_recv.at[0, lax.rem(c, 4)], sib)

    def st2(c):
        return rcopy(s1.at[lax.rem(c, 2)], rx1.at[lax.rem(c, 4)], d_send.at[1, lax.rem(c, 2)], d_recv.at[1, lax.rem(c, 4)], dev1)

    def st3(c):
        return rcopy(s2.at[lax.rem(c, 2)], rx2.at[c], d_send.at[2, lax.rem(c, 2)], d_recv.at[2, c], dev2)

    def st4(c):
        return rcopy(s3.at[lax.rem(c, 2)], rx3.at[c], d_send.at[3, lax.rem(c, 2)], d_recv.at[3, c], sib)

    def refill(c, grp):
        @pl.when(c + 1 < nc)
        def _():
            for j in grp:
                load_down(c + 1, j).start()

    def down(c, grp):
        for j in grp:
            load_down(c, j).wait()
        outs = [jnp.dot(act[e], wb[e], preferred_element_type=F32).astype(BF) for e in grp]
        for e, o in zip(grp, outs):
            for p in range(4):
                orow[p, e * 2 * CAP:(e + 1) * 2 * CAP, :] = o[p * 2 * CAP:(p + 1) * 2 * CAP]
        refill(c, grp)

    def combine(c):
        sl = lax.rem(c, 2)
        for dy in (1, 0):
            for dx in (1, 0):
                py = (1 - cy) if dy else cy
                px = (1 - cx) if dx else cx
                p = py * 2 + px
                r3 = jnp.dot(cm[p], orow[p], preferred_element_type=F32)
                res = r3[0:256] + r3[256:512] + r3[512:768]
                for h in range(2):
                    a, b = (dx, dy) if h == 0 else (dy, dx)
                    for cc in range(2):
                        part[sl, h, a, b, cc ^ h] = res[cc * 128:(cc + 1) * 128, h * 128:(h + 1) * 128]
        st1(c).start()

    def shared_down(c):
        cols = pl.ds(pl.multiple_of(c * CW, CW), CW)
        grp = (n_loc, n_loc + 1)
        for j in grp:
            load_down(c, j).wait()
        sh = (jnp.dot(act_sh[:, :inter], wb[n_loc], preferred_element_type=F32)
              + jnp.dot(act_sh[:, inter:], wb[n_loc + 1], preferred_element_type=F32))
        ybase[:, cols] = h1_ref[:, cols].astype(F32) + sh
        refill(c, grp)

    def stage2(k):
        sl = lax.rem(k, 2)
        st1(k).wait_recv()

        @pl.when(k >= 2)
        def _():
            st2(k - 2).wait_send()
        for b in range(2):
            for d in range(2):
                s1[sl, b, d] = part[sl, core, 1, b, d] + rx0[lax.rem(k, 4), 1, b, d]
        st2(k).start()
        for b in range(2):
            for d in range(2):
                keep0[sl, b, d] = part[sl, core, 0, b, d] + rx0[lax.rem(k, 4), 0, b, d]
        st1(k).wait_send()

    def stage3(k):
        sl = lax.rem(k, 2)
        st2(k).wait_recv()

        @pl.when(k >= 2)
        def _():
            st3(k - 2).wait_send()
        for d in range(2):
            s2[sl, d] = keep0[sl, 1, d] + rx1[lax.rem(k, 4), 1, d]
        st3(k).start()
        for d in range(2):
            keep1[sl, d] = keep0[sl, 0, d] + rx1[lax.rem(k, 4), 0, d]

    def stage4(k):
        sl = lax.rem(k, 2)
        st3(k).wait_recv()

        @pl.when(k >= 2)
        def _():
            st4(k - 2).wait_send()
        s3[sl] = keep1[sl, 1] + rx2[k, 1]
        st4(k).start()
        keep2[sl] = keep1[sl, 0] + rx2[k, 0]

    def stage5(k):
        mine = pl.ds(pl.multiple_of(k * CW + core * 128, 128), 128)
        other = pl.ds(pl.multiple_of(k * CW + (1 - core) * 128, 128), 128)
        st4(k).wait_recv()
        y_ref[:, mine] = (ybase[:, mine] + keep2[lax.rem(k, 2)]).astype(BF)
        y_ref[:, other] = (ybase[:, other] + rx3[k]).astype(BF)

    def chunk(c, carry):
        live = c < nc
        pl.when(live)(lambda: down(c, (0, 1, 2, 3)))
        pl.when(jnp.logical_and(c >= 1, c < nc + 1))(lambda: stage2(c - 1))
        pl.when(live)(lambda: down(c, (4, 5, 6, 7)))
        pl.when(jnp.logical_and(c >= 2, c < nc + 2))(lambda: stage3(c - 2))
        pl.when(live)(lambda: combine(c))
        pl.when(live)(lambda: shared_down(c))
        pl.when(jnp.logical_and(c >= 3, c < nc + 3))(lambda: stage4(c - 3))
        pl.when(c >= 4)(lambda: stage5(c - 4))
        return carry

    lax.fori_loop(0, nc + 4, chunk, 0)
    for k in (nc - 2, nc - 1):
        st2(k).wait_send()
        st3(k).wait_send()
        st4(k).wait_send()


def moe(u, h1, wt, s_gate, s_up, s_down, e_gate, e_up, e_down):
    t, hid = u.shape
    n_loc, _, inter = e_gate.shape
    nc = hid // CW
    V = pltpu.VMEM
    D = pltpu.SemaphoreType.DMA
    vm = pl.BlockSpec(memory_space=pltpu.VMEM)
    an = pl.BlockSpec(memory_space=pl.ANY)
    return pl.pallas_call(
        moe_kernel,
        out_shape=jax.ShapeDtypeStruct((t, hid), BF),
        in_specs=[vm] * 3 + [an] * 6,
        out_specs=vm,
        scratch_shapes=[
            V((8, t, hid), BF), V((8, n_loc, t), F32), V((8, n_loc, t), F32), V((n_loc * 2 * CAP, 256), F32),
            V((4, n_loc * 2 * CAP, 256), BF), V((4, 768, n_loc * 2 * CAP), BF),
            V((n_loc, 8 * CAP, hid), BF), V((n_loc, 8 * CAP, inter), BF), V((t, 2 * inter), BF),
            V((4, n_loc * 2 * CAP, CW), BF),
            V((2, 2, hid, NA), BF), V((2, 2, hid, inter - NA), BF), V((n_loc + 2, inter, CW), BF), V((t, hid), F32),
            V((2, 2, 2, 2, 2, t, 128), F32), V((4, 2, 2, 2, t, 128), F32), V((4, 2, 2, t, 128), F32),
            V((nc, 2, t, 128), F32), V((nc, t, 128), F32),
            V((2, 2, 2, t, 128), F32), V((2, 2, 2, t, 128), F32),
            V((2, 2, t, 128), F32), V((2, 2, t, 128), F32), V((2, t, 128), F32), V((2, t, 128), F32),
            D((2, 2, 2)), D((n_loc + 2,)), D((8,)), D((8,)), D((7, NSUB)), D((8, NSUB)),
            D((4, 2)), D((4, nc)),
        ],
        compiler_params=pltpu.CompilerParams(collective_id=0, has_side_effects=True, vmem_limit_bytes=67043328),
        name='moe',
    )(u, h1, wt, s_gate, s_up, s_down, e_gate, e_up, e_down)


def solution(mesh):
    tok_spec = P(('rep', 'ep'))
    row_spec = P(('rep', 'ep'), None)
    cache_spec = P(('rep', 'ep'), None, None)
    exp_spec = P('ep', None, None)

    def local(x, cache, lens, ids, rw, w_q, w_dkv, w_uk, w_uv, w_o, s_gate, s_up, s_down, e_gate, e_up, e_down):
        n_exp = e_gate.shape[0] * mesh.shape['ep']
        h1, u, kv_new, wt = attention(x, cache, lens, ids, rw, n_exp, w_q, w_dkv, w_uk, w_uv, w_o)
        y = moe(u, h1, wt, s_gate, s_up, s_down, e_gate, e_up, e_down)
        return y, kv_new

    in_specs = (row_spec, cache_spec, tok_spec, row_spec, row_spec) + (P(),) * 8 + (exp_spec,) * 3
    return jax.shard_map(local, mesh=mesh, in_specs=in_specs, out_specs=(row_spec, row_spec), check_vma=False)
```

time: 188 us -> 136 us (0.72)
  matrix products: 55.2 us -> 0 us
  Pallas kernels: 116 us -> 131 us
  other arithmetic: 8.56 us -> 1.64 us
  local copies, waits for them, and re-layouts: 6.29 us -> 1.88 us
    dot_general x8 -> x0, matrix products: 55.2 us -> none  [the longest x1 16.9 us: attention(): jnp.einsum('bhc,blc->bhl', qf, cache, preferred_element_type=jnp.float32)]
    pallas_call x0 -> x1, Pallas kernels: none -> 30.3 us  [attention(): pl.pallas_call(attn_kernel, out_shape=(jax.ShapeDtypeStruct((t, hid), BF)...]
    pallas_call x1, Pallas kernels: 116 us -> 101 us  [moe(): pl.pallas_call(moe_kernel, out_shape=jax.ShapeDtypeStruct((t, hid), BF),...]
    reduce_sum x4 -> x0, other arithmetic: 4.6 us -> none  [the longest x1 2.59 us: attention(): den = jnp.sum(e, axis=2) + e_new]
    unnamed x24 -> x1, local copies, waits for them, and re-layouts: 4.66 us -> 1.88 us
    concatenate x3 -> x0, other arithmetic: 2.13 us -> none  [the longest x2 1.62 us: attention(): jnp.concatenate([rms(kv[:, :kvl]), rope(kv[:, kvl:], lens)], axis=-1)]
where the time goes in v2:
time: 136 us
  Pallas kernels  131 us (96%)
  local copies, waits for them, and re-layouts  1.88 us (1%)
  other arithmetic  1.64 us (1%)
    pallas_call x1, Pallas kernels, moe(): pl.pallas_call(moe_kernel, out_shape=jax.ShapeDtypeStruct((t, hid), BF),...  101 us
    pallas_call x1, Pallas kernels, attention(): pl.pallas_call(attn_kernel, out_shape=(jax.ShapeDtypeStruct((t, hid), BF)...  30.3 us

profile of v2, /device:TPU:0, one launch (start us, length us, event | category | flops | bytes accessed | tf_op | source)
XLA Modules:
  0.0 135.7 jit_solution(14895892130179654008)
XLA Ops:
  0.6 0.7 convert_element_type.10
  1.3 1.0 fusion
  2.3 30.3 %attn.1 = (bf16[128,2048]{1,0:T(8,128)(2,1)}, bf16[128,2048]{1,0:T(8,128)(2,1)}, bf16[576,128]{1,0:T(8,128)(2,1)}, f32[64,128]{1,0:T(8,128)}) custom-call(s32[128]{0:T(128)} %lens_ref.1, s32[6,128]{1,0:T(8,128)} %bitcast.7, f32[6,128]{1,0:T(8,128)} %bitcast.8, bf16[128,2048]{1,0:T(8,128)(2,1)} %x_ref.1, f32[128,128]{1,0:T(8,128)} %get-tuple-element.11.cs_ref, ...), custom_call_target="tpu_custom_call" | custom-call | tf_op jit(solution)/shard_map/attn/pallas_call | solution.py:163
  32.6 101.2 %moe.1 = bf16[128,2048]{1,0:T(8,128)(2,1)} custom-call(bf16[128,2048]{1,0:T(8,128)(2,1)} %get-tuple-element.6.u_ref, bf16[128,2048]{1,0:T(8,128)(2,1)} %get-tuple-element.7.h1_ref, f32[64,128]{1,0:T(8,128)} %get-tuple-element.8.wt_ref, bf16[2048,2816]{1,0:T(8,128)(2,1)} %sg.1, bf16[2048,2816]{1,0:T(8,128)(2,1)} %su.1, bf16[2816,2048]{1,0:T(8,128)(2,1)} %sd.1, ...), custom_call_target="tpu_custom_call" | custom-call | tf_op jit(solution)/shard_map/moe/pallas_call | solution.py:502
  133.8 1.9 %copy.19 = bf16[128,2048]{1,0:T(8,128)(2,1)} copy(bf16[128,2048]{1,0:T(8,128)(2,1)} %moe.1) | data formatting | bytes 1048576
  (1 shorter events, 0.0 us)

commit v3 on v0

v3 whole, which is shorter than its diff:
```python
import jax
import jax.numpy as jnp
from jax import lax
from jax.experimental import pallas as pl
from jax.experimental.pallas import tpu as pltpu
from jax.sharding import PartitionSpec as P

EPS = 1e-6
ROPE_BASE = 1.0e4
BF = jnp.bfloat16
F32 = jnp.float32
CAP = 24
CW = 256
NA = 768
NSUB = 4


NB = 16
RING = 2
CW = 256
NA = 768
NSUB = 4


def layer_kernel(lens_ref, ids_ref, rw_ref, x_ref, cs_ref, sn_ref, wq_h, wdkv_h, wuk_h, wuv_h, wo_h, cache_h,
                 sg, su, sd, eg, eu, ed,
                 y_ref, kvn_ref,
                 u_all, wt_ref, wt_all, h1_ref, wa, wc0, rx0, rx1, rx2, rx3,
                 sem_w, sem_q, sem_c, sem_a, sem_b, wt_send, wt_recv, g_send, g_recv, d_send, d_recv):
    n = 8
    n_loc = eg.shape[0]
    t, hid = x_ref.shape
    inter = eg.shape[2]
    nc = hid // CW
    na = NA
    rsub = t // NSUB
    me = lax.axis_index('ep')
    core = lax.rem(me, 2)
    chip = me // 2
    cx = lax.rem(chip, 2)
    cy = chip // 2
    sib = chip * 2 + 1 - core
    xn_ = (cy * 2 + 1 - cx) * 2 + core
    yn_ = ((1 - cy) * 2 + cx) * 2 + core
    dg = ((1 - cy) * 2 + 1 - cx) * 2 + core
    dev1 = xn_ * (1 - core) + yn_ * core
    dev2 = yn_ * (1 - core) + xn_ * core

    def rcopy(src, dst, ssem, rsem, dev):
        return pltpu.make_async_remote_copy(src_ref=src, dst_ref=dst, send_sem=ssem, recv_sem=rsem,
                                            device_id={'ep': dev}, device_id_type=pl.DeviceIdType.MESH)

    def ucopy(kind, s, i, dev):
        rows = pl.ds(i * rsub, rsub)
        return rcopy(u_all.at[s, rows], u_all.at[s, rows], g_send.at[kind, i], g_recv.at[s, i], dev)

    def arrive(s, subs=range(NSUB)):
        for i in subs:
            ucopy(0, s, i, sib).wait_recv()

    def partner(s):
        return (s // 2) * 2 + 1 - lax.rem(s, 2)

    def wt_copy(k):
        d = lax.rem(me + k, n)
        return rcopy(wt_ref.at[pl.ds(pl.multiple_of(d * n_loc, n_loc), n_loc)], wt_all.at[me],
                     wt_send.at[k], wt_recv.at[me], d)

    def relay(kinds, s, devs, subs):
        for i in subs:
            arrive(s, (i,))
            for kind, dev in zip(kinds, devs):
                cp = ucopy(kind, s, i, dev)
                cp.start()

    def load_unit(srcs, base, slot, part_, wc1):
        if part_ == 0:
            dst, width, off = [wa.at[2 * slot], wa.at[2 * slot + 1]], na, 0
        else:
            buf = wc1 if slot else wc0
            dst, width, off = [buf.at[0], buf.at[1]], inter - na, na
        return [pltpu.make_async_copy(src.at[:, pl.ds(base + off, width)], d, sem_a.at[part_, slot, i])
                for i, (src, d) in enumerate(zip(srcs, dst))]

    def load_shared(half, part_, wc1=None):
        return load_unit((sg, su), half * inter, half, part_, wc1)

    def relay_near(i):
        relay((3, 4), dev1, (dev2, sib), (i,))
        relay((5,), dev2, (sib,), (i,))

    na_blk = t * 3 // 4 // NB

    def attn_scope(wdkv, wuk, wuv, wo, cbuf, qs, kvs, os, oc):
        heads, nope, kvl = wuk.shape
        kvd = cbuf.shape[2]
        rot = kvd - kvl
        qkd = nope + rot
        length = cbuf.shape[3]
        vh = wuv.shape[2]
        nblk = t // NB
        qw = 4 * qkd
        nq = heads // 4
        scale = qkd ** -0.5

        cp_dkv = pltpu.make_async_copy(wdkv_h, wdkv, sem_w.at[0])
        cp_uk = pltpu.make_async_copy(wuk_h, wuk, sem_w.at[1])
        cp_uv = pltpu.make_async_copy(wuv_h, wuv, sem_w.at[2])
        cp_o = pltpu.make_async_copy(wo_h, wo, sem_w.at[3])
        cp_q = [pltpu.make_async_copy(wq_h.at[:, i * qw:(i + 1) * qw], wa.at[i], sem_q.at[i]) for i in range(nq)]

        def load(b):
            sl = lax.rem(b, RING)
            return pltpu.make_async_copy(cache_h.at[pl.ds(b * NB, NB)], cbuf.at[sl], sem_c.at[sl])

        cp_dkv.start()
        cp_q[0].start()
        cp_uk.start()
        for cp in cp_q[1:]:
            cp.start()
        for b in range(RING):
            load(b).start()
        cp_uv.start()
        cp_o.start()

        barrier = pltpu.get_barrier_semaphore()
        for k in range(1, n):
            pl.semaphore_signal(barrier, inc=1, device_id={'ep': lax.rem(me + k, n)}, device_id_type=pl.DeviceIdType.MESH)
        pl.semaphore_wait(barrier, n - 1)

        ex = lax.broadcasted_iota(jnp.int32, wt_ref.shape, 0)
        wt = jnp.zeros(wt_ref.shape, F32)
        for k in range(ids_ref.shape[0]):
            wt = wt + jnp.where(ids_ref[k:k + 1, :] == ex, rw_ref[k:k + 1, :], 0.0)
        wt_ref[...] = wt
        wt_all[me] = wt_ref[pl.ds(pl.multiple_of(me * n_loc, n_loc), n_loc), :]
        cs = cs_ref[...]
        sn = sn_ref[...]
        lane = lax.broadcasted_iota(jnp.int32, (t, 128), 1)
        low = lax.rem(lane, rot) < rot // 2

        def rope2(v):
            sw = jnp.where(low, pltpu.roll(v, 128 - rot // 2, 1), pltpu.roll(v, rot // 2, 1))
            return v * cs + sw * sn

        xf = x_ref[...].astype(F32)
        xn = (xf * lax.rsqrt(jnp.mean(xf * xf, axis=-1, keepdims=True) + EPS)).astype(BF)

        cp_dkv.wait()
        kv = lax.dot_general(xn, wdkv[...], (((1,), (1,)), ((), ())), preferred_element_type=F32)
        kl = kv[:, 0:kvl]
        kl = (kl * lax.rsqrt(jnp.mean(kl * kl, axis=-1, keepdims=True) + EPS)).astype(BF)
        kr = kv[:, kvl:kvd]
        kr = rope2(jnp.concatenate([kr, kr], axis=1)).astype(BF)
        kvs[:, 0:kvl] = kl.astype(F32)
        kvs[:, kvl:kvl + 128] = jnp.where(lane < rot, kr.astype(F32), 0.0)
        kvn_ref[...] = kvs[...].T[0:kvd].astype(BF)

        for k in range(1, n):
            wt_copy(k).start()

        for i in range(nq):
            cp_q[i].wait()
            qc = jnp.dot(xn, wa[i], preferred_element_type=F32).astype(BF).astype(F32)
            if i == 0:
                cp_uk.wait()
            for j in range(2):
                o0 = j * 2 * qkd
                h = i * 4 + j * 2
                n0 = qc[:, o0:o0 + nope].astype(BF)
                n1 = qc[:, o0 + qkd:o0 + qkd + nope].astype(BF)
                r = jnp.concatenate([qc[:, o0 + nope:o0 + qkd], qc[:, o0 + qkd + nope:o0 + 2 * qkd]], axis=1)
                r = rope2(r).astype(BF).astype(F32)
                qs[:, h, 0:kvl] = jnp.dot(n0, wuk[h], preferred_element_type=F32).astype(BF).astype(F32)
                qs[:, h + 1, 0:kvl] = jnp.dot(n1, wuk[h + 1], preferred_element_type=F32).astype(BF).astype(F32)
                qs[:, h, kvl:kvl + 128] = jnp.where(lane < rot, r, 0.0)
                qs[:, h + 1, kvl:kvl + 128] = jnp.where(lane < rot, pltpu.roll(r, rot, 1), 0.0)

        pos = lax.broadcasted_iota(jnp.int32, (heads, length), 1)

        def block(b, carry):
            sl = lax.rem(b, RING)
            load(b).wait()
            ss = []
            sns = []
            for i in range(NB):
                qf = qs[b * NB + i]
                qb = qf[:, 0:kvd].astype(BF)
                ss.append(jnp.dot(qb, cbuf[sl, i], preferred_element_type=F32))
                sns.append(jnp.sum(qf * kvs[pl.ds(b * NB + i, 1), :], axis=1, keepdims=True) * scale)
            for i in range(NB):
                s = jnp.where(pos < lens_ref[b * NB + i], ss[i] * scale, -jnp.inf)
                mx = jnp.maximum(jnp.max(s, axis=1, keepdims=True), sns[i])
                e = jnp.exp(s - mx)
                en = jnp.exp(sns[i] - mx)
                den = jnp.sum(e, axis=1, keepdims=True) + en
                p = (e / den).astype(BF)
                pn = (en / den).astype(BF).astype(F32)
                o = lax.dot_general(p, cbuf[sl, i, 0:kvl, :], (((1,), (1,)), ((), ())), preferred_element_type=F32)
                os[:, lax.rem(b, na_blk) * NB + i, :] = o + pn * kvs[pl.ds(b * NB + i, 1), 0:kvl]

            @pl.when(b + RING < nblk)
            def _():
                load(b + RING).start()

            for j, cp in enumerate(load_shared(0, 0) + load_shared(1, 0) + load_shared(0, 1)):
                pl.when(b == j + 2)(cp.start)
            return carry

        for half in range(2):
            lax.fori_loop((0, na_blk)[half], (na_blk, nblk)[half], block, 0)
            if half == 0:
                cp_uv.wait()
                cp_o.wait()
            else:
                relay_near(0)
            rows = slice((0, na_blk * NB)[half], (na_blk * NB, t)[half])
            nh = rows.stop - rows.start
            for h in range(heads):
                oc[0:nh, h * vh:(h + 1) * vh] = jnp.dot(os[h, 0:nh].astype(BF), wuv[h], preferred_element_type=F32).astype(BF)
            ssq = jnp.zeros((nh, 1), F32)
            for a in range(0, hid, 512):
                h1 = (x_ref[rows, a:a + 512].astype(F32)
                      + jnp.dot(oc[0:nh], wo[:, a:a + 512], preferred_element_type=F32)).astype(BF)
                h1_ref[rows, a:a + 512] = h1
                hf = h1.astype(F32)
                ssq = ssq + jnp.sum(hf * hf, axis=1, keepdims=True)
            inv = lax.rsqrt(ssq * (1.0 / hid) + EPS)
            u_all[me, rows, :] = (h1_ref[rows, :].astype(F32) * inv).astype(BF)
            for i in range(rows.start // rsub, rows.stop // rsub):
                for kind, d in enumerate((dev1, dev2, sib)):
                    cp = ucopy(kind, me, i, d)
                    cp.start()

    heads, nope, kvl = wuk_h.shape
    vh = wuv_h.shape[2]
    _, kvd, length = cache_h.shape
    V = pltpu.VMEM
    pl.run_scoped(
        attn_scope,
        V((kvd, hid), BF), V((heads, nope, kvl), BF),
        V((heads, kvl, vh), BF), V((heads * vh, hid), BF), V((RING, NB, kvd, length), BF),
        V((t, heads, kvl + 128), F32), V((t, kvl + 128), F32), V((heads, na_blk * NB, kvl), F32), V((na_blk * NB, heads * vh), BF))

    def moe_scope(rank_s, wsel, pm, cm, xr, act, act_sh, orow, wc1, wb, ybase,
                  part, s1, keep0, s2, keep1, s3, keep2):
        def load_expert(e, slot, part_):
            return load_unit((eg.at[e], eu.at[e]), 0, slot, part_, wc1)

        def load_routed(c, e):
            cols = pl.ds(pl.multiple_of(c * CW, CW), CW)
            return pltpu.make_async_copy(ed.at[e, :, cols], wb.at[e], sem_b.at[e])

        def load_down(c, j):
            cols = pl.ds(pl.multiple_of(c * CW, CW), CW)
            if j < n_loc:
                src = ed.at[j, :, cols]
            else:
                src = sd.at[pl.ds((j - n_loc) * inter, inter), cols]
            return pltpu.make_async_copy(src, wb.at[j], sem_b.at[j])

        for cp in load_shared(1, 1, wc1):
            cp.start()
        relay_near(1)

        def glu(lhs, gw, uw):
            g = jnp.dot(lhs, gw, preferred_element_type=F32)
            v = jnp.dot(lhs, uw, preferred_element_type=F32)
            return (g * (1.0 / (1.0 + jnp.exp(-g))) * v).astype(BF)

        def glu_unit(lhs, slot, part_, store):
            width, off = (na, 0) if part_ == 0 else (inter - na, na)
            for a in range(0, width, 256):
                b = min(a + 256, width)
                if part_ == 0:
                    gw, uw = wa[2 * slot, :, a:b], wa[2 * slot + 1, :, a:b]
                else:
                    buf = wc1 if slot else wc0
                    gw, uw = buf[0, :, a:b], buf[1, :, a:b]
                store(off + a, off + b, glu(lhs, gw, uw))

        for half, part_ in ((0, 0), (1, 0), (0, 1), (1, 1)):
            for cp in load_shared(half, part_, wc1):
                cp.wait()

            def put(a, b, v):
                act_sh[:, half * inter + a:half * inter + b] = v

            glu_unit(u_all[me], half, part_, put)
            for cp in load_expert(half, half, part_):
                cp.start()
            if (half, part_) == (1, 0):
                relay_near(2)
        for j in range(n_loc + 2):
            load_down(0, j).start()
        relay((6,), dg, (sib,), (0,))
        for k in range(1, n):
            s = lax.rem(me + k, n)
            rcopy(wt_all.at[s], wt_all.at[s], wt_send.at[0], wt_recv.at[s], sib).wait_recv()
        w_all = wt_all[...].reshape(n * n_loc, 128)
        ti = lax.broadcasted_iota(jnp.int32, (128, 128), 0)
        tj = lax.broadcasted_iota(jnp.int32, (128, 128), 1)
        tri = (ti < tj).astype(F32).astype(BF)
        hit = w_all > 0.0
        rank = jnp.dot(hit.astype(F32).astype(BF), tri, preferred_element_type=F32)
        rank_s[...] = jnp.where(hit, rank, -1000.0).reshape(n, n_loc, 128)
        row48 = lax.broadcasted_iota(jnp.int32, (2 * CAP, 256), 0).astype(F32)

        def tables(p, carry):
            for e in range(n_loc):
                rk = jnp.concatenate([rank_s[2 * p, e:e + 1, :], rank_s[2 * p + 1, e:e + 1, :] + float(CAP)], axis=1)
                ww = jnp.concatenate([wt_all[2 * p, e:e + 1, :], wt_all[2 * p + 1, e:e + 1, :]], axis=1)
                sel = row48 == rk
                pm[p, e * 2 * CAP:(e + 1) * 2 * CAP, :] = jnp.where(sel, 1.0, 0.0).astype(BF)
                wsel[e * 2 * CAP:(e + 1) * 2 * CAP, :] = jnp.where(sel, ww, 0.0)
            wt = wsel[...].T
            b1 = wt.astype(BF)
            r1 = wt - b1.astype(F32)
            b2 = r1.astype(BF)
            b3 = (r1 - b2.astype(F32)).astype(BF)
            cm[p, 0:256, :] = b1
            cm[p, 256:512, :] = b2
            cm[p, 512:768, :] = b3
            return carry

        lax.fori_loop(0, 4, tables, 0)

        relay_near(3)
        relay((6,), dg, (sib,), (1, 2))

        def dispatch(p):
            rows = pl.ds(pl.multiple_of(p * 2 * CAP, 16), 2 * CAP)
            for a in range(0, hid, 512):
                uv = u_all[pl.ds(2 * p, 2), :, a:a + 512].reshape(256, 512)
                r = jnp.dot(pm[p], uv, preferred_element_type=F32).astype(BF)
                for e in range(n_loc):
                    xr[e, rows, a:a + 512] = r[e * 2 * CAP:(e + 1) * 2 * CAP]

        arrive(sib)
        dispatch(chip)
        arrive(partner(dev1))
        dispatch(dev1 // 2)
        arrive(partner(dev2))
        dispatch(dev2 // 2)
        relay((6,), dg, (sib,), (3,))
        arrive(partner(dg))
        dispatch(dg // 2)

        def gate_up(k, carry):
            for slot in range(2):
                e = 2 * k + slot

                def put(a, b, v):
                    act[e, :, a:b] = v

                for part_ in range(2):
                    for cp in load_expert(e, slot, part_):
                        cp.wait()
                    glu_unit(xr[e], slot, part_, put)

                    @pl.when(e + 2 < n_loc)
                    def _():
                        for cp in load_expert(e + 2, slot, part_):
                            cp.start()

            for slot in range(2):
                load_routed(0, 2 * k + slot).wait()
            outs = [jnp.dot(act[2 * k + slot], wb[2 * k + slot], preferred_element_type=F32).astype(BF) for slot in range(2)]
            for slot, o in enumerate(outs):
                rows = pl.ds(pl.multiple_of((2 * k + slot) * 2 * CAP, 16), 2 * CAP)
                for p in range(4):
                    orow[p, rows, :] = o[p * 2 * CAP:(p + 1) * 2 * CAP]

            @pl.when(k == n_loc // 2 - 2)
            def _():
                for j in range(n_loc - 2):
                    load_down(1, j).start()

            @pl.when(k == n_loc // 2 - 1)
            def _():
                for j in range(n_loc - 2, n_loc):
                    load_down(1, j).start()
            return carry

        lax.fori_loop(0, n_loc // 2, gate_up, 0)

        for i in range(NSUB):
            for kind, (s, d) in enumerate(((me, dev1), (me, dev2), (me, sib), (dev1, dev2), (dev1, sib), (dev2, sib), (dg, sib))):
                ucopy(kind, s, i, d).wait_send()
        for k in range(1, n):
            wt_copy(k).wait_send()

        def st1(c):
            return rcopy(part.at[lax.rem(c, 2), 1 - core], rx0.at[lax.rem(c, 4)], d_send.at[0, lax.rem(c, 2)], d_recv.at[0, lax.rem(c, 4)], sib)

        def st2(c):
            return rcopy(s1.at[lax.rem(c, 2)], rx1.at[lax.rem(c, 4)], d_send.at[1, lax.rem(c, 2)], d_recv.at[1, lax.rem(c, 4)], dev1)

        def st3(c):
            return rcopy(s2.at[lax.rem(c, 2)], rx2.at[c], d_send.at[2, lax.rem(c, 2)], d_recv.at[2, c], dev2)

        def st4(c):
            return rcopy(s3.at[lax.rem(c, 2)], rx3.at[c], d_send.at[3, lax.rem(c, 2)], d_recv.at[3, c], sib)

        def refill(c, grp):
            @pl.when(c + 1 < nc)
            def _():
                for j in grp:
                    load_down(c + 1, j).start()

        def down(c, grp):
            for j in grp:
                load_down(c, j).wait()
            outs = [jnp.dot(act[e], wb[e], preferred_element_type=F32).astype(BF) for e in grp]
            for e, o in zip(grp, outs):
                for p in range(4):
                    orow[p, e * 2 * CAP:(e + 1) * 2 * CAP, :] = o[p * 2 * CAP:(p + 1) * 2 * CAP]
            refill(c, grp)

        def combine(c):
            sl = lax.rem(c, 2)
            for dy in (1, 0):
                for dx in (1, 0):
                    py = (1 - cy) if dy else cy
                    px = (1 - cx) if dx else cx
                    p = py * 2 + px
                    r3 = jnp.dot(cm[p], orow[p], preferred_element_type=F32)
                    res = r3[0:256] + r3[256:512] + r3[512:768]
                    for h in range(2):
                        a, b = (dx, dy) if h == 0 else (dy, dx)
                        for cc in range(2):
                            part[sl, h, a, b, cc ^ h] = res[cc * 128:(cc + 1) * 128, h * 128:(h + 1) * 128]
            st1(c).start()

        def shared_down(c):
            cols = pl.ds(pl.multiple_of(c * CW, CW), CW)
            grp = (n_loc, n_loc + 1)
            for j in grp:
                load_down(c, j).wait()
            sh = (jnp.dot(act_sh[:, :inter], wb[n_loc], preferred_element_type=F32)
                  + jnp.dot(act_sh[:, inter:], wb[n_loc + 1], preferred_element_type=F32))
            ybase[:, cols] = h1_ref[:, cols].astype(F32) + sh
            refill(c, grp)

        def stage2(k):
            sl = lax.rem(k, 2)
            st1(k).wait_recv()

            @pl.when(k >= 2)
            def _():
                st2(k - 2).wait_send()
            for b in range(2):
                for d in range(2):
                    s1[sl, b, d] = part[sl, core, 1, b, d] + rx0[lax.rem(k, 4), 1, b, d]
            st2(k).start()
            for b in range(2):
                for d in range(2):
                    keep0[sl, b, d] = part[sl, core, 0, b, d] + rx0[lax.rem(k, 4), 0, b, d]
            st1(k).wait_send()

        def stage3(k):
            sl = lax.rem(k, 2)
            st2(k).wait_recv()

            @pl.when(k >= 2)
            def _():
                st3(k - 2).wait_send()
            for d in range(2):
                s2[sl, d] = keep0[sl, 1, d] + rx1[lax.rem(k, 4), 1, d]
            st3(k).start()
            for d in range(2):
                keep1[sl, d] = keep0[sl, 0, d] + rx1[lax.rem(k, 4), 0, d]

        def stage4(k):
            sl = lax.rem(k, 2)
            st3(k).wait_recv()

            @pl.when(k >= 2)
            def _():
                st4(k - 2).wait_send()
            s3[sl] = keep1[sl, 1] + rx2[k, 1]
            st4(k).start()
            keep2[sl] = keep1[sl, 0] + rx2[k, 0]

        def stage5(k):
            mine = pl.ds(pl.multiple_of(k * CW + core * 128, 128), 128)
            other = pl.ds(pl.multiple_of(k * CW + (1 - core) * 128, 128), 128)
            st4(k).wait_recv()
            y_ref[:, mine] = (ybase[:, mine] + keep2[lax.rem(k, 2)]).astype(BF)
            y_ref[:, other] = (ybase[:, other] + rx3[k]).astype(BF)

        def chunk(c, carry):
            live = c < nc
            pl.when(jnp.logical_and(c >= 1, live))(lambda: down(c, (0, 1, 2, 3)))
            pl.when(jnp.logical_and(c >= 1, c < nc + 1))(lambda: stage2(c - 1))
            pl.when(jnp.logical_and(c >= 1, live))(lambda: down(c, (4, 5, 6, 7)))
            pl.when(live)(lambda: combine(c))
            pl.when(live)(lambda: shared_down(c))
            pl.when(jnp.logical_and(c >= 2, c < nc + 2))(lambda: stage3(c - 2))
            pl.when(jnp.logical_and(c >= 3, c < nc + 3))(lambda: stage4(c - 3))
            pl.when(c >= 4)(lambda: stage5(c - 4))
            return carry

        lax.fori_loop(0, nc + 4, chunk, 0)
        for k in (nc - 2, nc - 1):
            st2(k).wait_send()
            st3(k).wait_send()
            st4(k).wait_send()

    pl.run_scoped(
        moe_scope,
        V((n, n_loc, t), F32), V((n_loc * 2 * CAP, 256), F32),
        V((4, n_loc * 2 * CAP, 256), BF), V((4, 768, n_loc * 2 * CAP), BF),
        V((n_loc, 8 * CAP, hid), BF), V((n_loc, 8 * CAP, inter), BF), V((t, 2 * inter), BF),
        V((4, n_loc * 2 * CAP, CW), BF),
        V((2, hid, inter - NA), BF), V((n_loc + 2, inter, CW), BF), V((t, hid), F32),
        V((2, 2, 2, 2, 2, t, 128), F32),
        V((2, 2, 2, t, 128), F32), V((2, 2, 2, t, 128), F32),
        V((2, 2, t, 128), F32), V((2, 2, t, 128), F32), V((2, t, 128), F32), V((2, t, 128), F32))


def copy_kernel(a_ref, b_ref, y_ref, kv_ref):
    y_ref[...] = a_ref[...]
    kv_ref[...] = b_ref[...]


def layer(x, cache, lens, ids, rw, w_q, w_dkv, w_uk, w_uv, w_o, s_gate, s_up, s_down, e_gate, e_up, e_down):
    t, hid = x.shape
    heads, nope, kvl = w_uk.shape
    _, length, kvd = cache.shape
    n_loc = e_gate.shape[0]
    nc = hid // CW
    rot = kvd - kvl
    half = rot // 2
    lane = jnp.arange(128)
    ang = ((lens[:, None] * 128 + lane[None, :]) >> 7).astype(F32) * (ROPE_BASE ** (-2.0 * (lane % half).astype(F32) / rot))[None, :]
    cs4 = jnp.cos(ang)
    sn4 = jnp.sin(ang) * jnp.where(lane % rot < half, -1.0, 1.0)[None, :]
    V = pltpu.VMEM
    D = pltpu.SemaphoreType.DMA
    vm = pl.BlockSpec(memory_space=pltpu.VMEM)
    an = pl.BlockSpec(memory_space=pl.ANY)
    y, kvt = pl.pallas_call(
        layer_kernel,
        out_shape=(jax.ShapeDtypeStruct((t, hid), BF), jax.ShapeDtypeStruct((kvd, t), BF)),
        in_specs=[pl.BlockSpec(memory_space=pltpu.SMEM)] + [vm] * 5 + [an] * 12,
        out_specs=(vm, vm),
        scratch_shapes=[
            V((8, t, hid), BF), V((8 * n_loc, t), F32), V((8, n_loc, t), F32), V((t, hid), BF),
            V((4, hid, NA), BF), V((2, hid, e_gate.shape[2] - NA), BF),
            V((4, 2, 2, 2, t, 128), F32), V((4, 2, 2, t, 128), F32), V((nc, 2, t, 128), F32), V((nc, t, 128), F32),
            D((4,)), D((heads // 4,)), D((RING,)), D((2, 2, 2)), D((n_loc + 2,)), D((8,)), D((8,)),
            D((7, NSUB)), D((8, NSUB)), D((4, 2)), D((4, nc)),
        ],
        compiler_params=pltpu.CompilerParams(collective_id=0, has_side_effects=True, vmem_limit_bytes=67043328),
        name='layer',
    )(lens, ids.T, rw.T, x, cs4, sn4, w_q, w_dkv.T, w_uk, w_uv, w_o, cache.transpose(0, 2, 1),
      s_gate, s_up, s_down, e_gate, e_up, e_down)
    y, kvt = pl.pallas_call(
        copy_kernel,
        out_shape=(jax.ShapeDtypeStruct((t, hid), BF), jax.ShapeDtypeStruct((kvd, t), BF)),
        in_specs=[vm, vm],
        out_specs=(vm, vm),
        name='out',
    )(y, kvt)
    return y, kvt.T


def solution(mesh):
    tok_spec = P(('rep', 'ep'))
    row_spec = P(('rep', 'ep'), None)
    cache_spec = P(('rep', 'ep'), None, None)
    exp_spec = P('ep', None, None)
    in_specs = (row_spec, cache_spec, tok_spec, row_spec, row_spec) + (P(),) * 8 + (exp_spec,) * 3
    return jax.shard_map(layer, mesh=mesh, in_specs=in_specs, out_specs=(row_spec, row_spec), check_vma=False)
```

time: 316 us -> 124 us (0.39); the launches traced: 311 us -> 123 us
  matrix products: 152 us -> 0 us
  Pallas kernels: 0 us -> 121 us
  blocking collectives: 75.6 us -> 0 us
  waiting for transfers between devices: 58.1 us -> 0 us
  local copies, waits for them, and re-layouts: 13.2 us -> 0 us
  other arithmetic: 7.34 us -> 1.65 us
  starting transfers between devices: 3.86 us -> 0 us
    dot_general x17 -> x0, matrix products: 152 us -> none  [the longest x1 25.2 us: local(): v = jnp.einsum('erh,ehi->eri', xr, e_up, preferred_element_type=jnp.float32)]
    pallas_call x0 -> x2, Pallas kernels: none -> 121 us  [the longest x1 119 us: layer(): pl.pallas_call(layer_kernel, out_shape=(jax.ShapeDtypeStruct((t, hid), BF...]
    all_to_all x1 -> x0, blocking collectives: 75.6 us -> none  [local(): recv = lax.all_to_all(send, 'ep', 0, 0, tiled=True)]
    all_to_all x1 -> x0, waiting for transfers between devices: 58.1 us -> none  [local(): ret = lax.all_to_all(back, 'ep', 0, 0, tiled=True)]
    reshape x2 -> x0, local copies, waits for them, and re-layouts: 6.5 us -> none  [the longest x1 3.27 us: local(): recv.reshape(n, e_loc, cape, hid).transpose(1, 0, 2, 3)]
    convert_element_type x6 -> x0, local copies, waits for them, and re-layouts: 4.66 us -> none  [the longest x1 2.66 us: route(): jnp.einsum('jbke,bkr->jber', hw, at, preferred_element_type=jnp.float32)]
    all_to_all x1 -> x0, starting transfers between devices: 3.86 us -> none  [local(): ret = lax.all_to_all(back, 'ep', 0, 0, tiled=True)]
  transfers between devices with their start and end apart: 1 -> 0, of which waited for: 1 -> 0; matrix products, arithmetic and copies ran while one was open for 4% -> 0% of each run, Pallas kernels for 0% -> 0%
where the time goes in v3:
time: 124 us; the launch traced here: 123 us
  Pallas kernels  121 us (98%)
  other arithmetic  1.65 us (1%)
    pallas_call x1, Pallas kernels, layer(): pl.pallas_call(layer_kernel, out_shape=(jax.ShapeDtypeStruct((t, hid), BF...  119 us

profile of v3, /device:TPU:0, one launch (start us, length us, event | category | flops | bytes accessed | tf_op | source)
XLA Modules:
  0.0 123.5 jit_solution(11752278487692744998)
XLA Ops:
  0.6 0.7 broadcast_multiply_fusion
  1.3 1.0 sine_multiply_fusion
  2.3 119.2 %layer.1 = (bf16[128,2048]{1,0:T(8,128)(2,1)}, bf16[576,128]{1,0:T(8,128)(2,1)}) custom-call(s32[128]{0:T(128)} %lens_ref.1, s32[6,128]{1,0:T(8,128)} %bitcast.7, f32[6,128]{1,0:T(8,128)} %bitcast.8, bf16[128,2048]{1,0:T(8,128)(2,1)} %x_ref.1, f32[128,128]{1,0:T(8,128)} %get-tuple-element.11.cs_ref, f32[128,128]{1,0:T(8,128)} %get-tuple-element.10.sn_ref, ...), custom_call_target="tpu_custom_call" | custom-call | tf_op jit(solution)/shard_map/layer/pallas_call | solution.py:543
  121.5 1.9 %out.1 = (bf16[128,2048]{1,0:T(8,128)(2,1)}, bf16[576,128]{1,0:T(8,128)(2,1)}) custom-call(bf16[128,2048]{1,0:T(8,128)(2,1)} %get-tuple-element.6.a_ref, bf16[576,128]{1,0:T(8,128)(2,1)} %get-tuple-element.7.b_ref), custom_call_target="tpu_custom_call" | custom-call | tf_op jit(solution)/shard_map/out/pallas_call | solution.py:559
  (1 shorter events, 0.0 us)

commit v4 on v3

--- a/solution.py
+++ b/solution.py
@@ -1,5 +1,6 @@
 import jax
 import jax.numpy as jnp
+import numpy as np
 from jax import lax
 from jax.experimental import pallas as pl
 from jax.experimental.pallas import tpu as pltpu
@@ -10,9 +11,6 @@
 BF = jnp.bfloat16
 F32 = jnp.float32
 CAP = 24
-CW = 256
-NA = 768
-NSUB = 4
 
 
 NB = 16
@@ -20,9 +18,14 @@
 CW = 256
 NA = 768
 NSUB = 4
-
-
-def layer_kernel(lens_ref, ids_ref, rw_ref, x_ref, cs_ref, sn_ref, wq_h, wdkv_h, wuk_h, wuv_h, wo_h, cache_h,
+NT = (((1,), (1,)), ((), ()))
+SLOT = 2 * CAP
+LN = 128
+LAST = -1
+YES = True
+
+
+def layer_kernel(lens_ref, lrow_ref, inv_ref, ids_ref, rw_ref, x_ref, wq_h, wdkv_h, wuk_h, wuv_h, wo_h, cache_h,
                  sg, su, sd, eg, eu, ed,
                  y_ref, kvn_ref,
                  u_all, wt_ref, wt_all, h1_ref, wa, wc0, rx0, rx1, rx2, rx3,
@@ -134,9 +137,10 @@
             wt = wt + jnp.where(ids_ref[k:k + 1, :] == ex, rw_ref[k:k + 1, :], 0.0)
         wt_ref[...] = wt
         wt_all[me] = wt_ref[pl.ds(pl.multiple_of(me * n_loc, n_loc), n_loc), :]
-        cs = cs_ref[...]
-        sn = sn_ref[...]
         lane = lax.broadcasted_iota(jnp.int32, (t, 128), 1)
+        ang = jnp.broadcast_to(lrow_ref[...].astype(F32), (128, t)).T * inv_ref[...]
+        cs = jnp.cos(ang)
+        sn = jnp.where(lax.rem(lane, rot) < rot // 2, -jnp.sin(ang), jnp.sin(ang))
         low = lax.rem(lane, rot) < rot // 2
 
         def rope2(v):
@@ -144,17 +148,17 @@
             return v * cs + sw * sn
 
         xf = x_ref[...].astype(F32)
-        xn = (xf * lax.rsqrt(jnp.mean(xf * xf, axis=-1, keepdims=True) + EPS)).astype(BF)
+        xn = (xf * lax.rsqrt(jnp.mean(xf * xf, axis=LAST, keepdims=YES) + EPS)).astype(BF)
 
         cp_dkv.wait()
-        kv = lax.dot_general(xn, wdkv[...], (((1,), (1,)), ((), ())), preferred_element_type=F32)
-        kl = kv[:, 0:kvl]
-        kl = (kl * lax.rsqrt(jnp.mean(kl * kl, axis=-1, keepdims=True) + EPS)).astype(BF)
+        kv = lax.dot_general(xn, wdkv[...], NT, preferred_element_type=F32)
+        kl = kv[:, :kvl]
+        kl = (kl * lax.rsqrt(jnp.mean(kl * kl, axis=LAST, keepdims=YES) + EPS)).astype(BF)
         kr = kv[:, kvl:kvd]
         kr = rope2(jnp.concatenate([kr, kr], axis=1)).astype(BF)
-        kvs[:, 0:kvl] = kl.astype(F32)
-        kvs[:, kvl:kvl + 128] = jnp.where(lane < rot, kr.astype(F32), 0.0)
-        kvn_ref[...] = kvs[...].T[0:kvd].astype(BF)
+        kvs[:, :kvl] = kl.astype(F32)
+        kvs[:, kvl:kvl + LN] = jnp.where(lane < rot, kr.astype(F32), 0.0)
+        kvn_ref[...] = kvs[...].T[:kvd].astype(BF)
 
         for k in range(1, n):
             wt_copy(k).start()
@@ -171,10 +175,10 @@
                 n1 = qc[:, o0 + qkd:o0 + qkd + nope].astype(BF)
                 r = jnp.concatenate([qc[:, o0 + nope:o0 + qkd], qc[:, o0 + qkd + nope:o0 + 2 * qkd]], axis=1)
                 r = rope2(r).astype(BF).astype(F32)
-                qs[:, h, 0:kvl] = jnp.dot(n0, wuk[h], preferred_element_type=F32).astype(BF).astype(F32)
-                qs[:, h + 1, 0:kvl] = jnp.dot(n1, wuk[h + 1], preferred_element_type=F32).astype(BF).astype(F32)
-                qs[:, h, kvl:kvl + 128] = jnp.where(lane < rot, r, 0.0)
-                qs[:, h + 1, kvl:kvl + 128] = jnp.where(lane < rot, pltpu.roll(r, rot, 1), 0.0)
+                qs[:, h, :kvl] = jnp.dot(n0, wuk[h], preferred_element_type=F32).astype(BF).astype(F32)
+                qs[:, h + 1, :kvl] = jnp.dot(n1, wuk[h + 1], preferred_element_type=F32).astype(BF).astype(F32)
+                qs[:, h, kvl:kvl + LN] = jnp.where(lane < rot, r, 0.0)
+                qs[:, h + 1, kvl:kvl + LN] = jnp.where(lane < rot, pltpu.roll(r, rot, 1), 0.0)
 
         pos = lax.broadcasted_iota(jnp.int32, (heads, length), 1)
 
@@ -187,17 +191,17 @@
                 qf = qs[b * NB + i]
                 qb = qf[:, 0:kvd].astype(BF)
                 ss.append(jnp.dot(qb, cbuf[sl, i], preferred_element_type=F32))
-                sns.append(jnp.sum(qf * kvs[pl.ds(b * NB + i, 1), :], axis=1, keepdims=True) * scale)
+                sns.append(jnp.sum(qf * kvs[pl.ds(b * NB + i, 1), :], axis=LAST, keepdims=YES) * scale)
             for i in range(NB):
                 s = jnp.where(pos < lens_ref[b * NB + i], ss[i] * scale, -jnp.inf)
-                mx = jnp.maximum(jnp.max(s, axis=1, keepdims=True), sns[i])
+                mx = jnp.maximum(jnp.max(s, axis=LAST, keepdims=YES), sns[i])
                 e = jnp.exp(s - mx)
                 en = jnp.exp(sns[i] - mx)
-                den = jnp.sum(e, axis=1, keepdims=True) + en
+                den = jnp.sum(e, axis=LAST, keepdims=YES) + en
                 p = (e / den).astype(BF)
                 pn = (en / den).astype(BF).astype(F32)
-                o = lax.dot_general(p, cbuf[sl, i, 0:kvl, :], (((1,), (1,)), ((), ())), preferred_element_type=F32)
-                os[:, lax.rem(b, na_blk) * NB + i, :] = o + pn * kvs[pl.ds(b * NB + i, 1), 0:kvl]
+                o = lax.dot_general(p, cbuf[sl, i, :kvl, :], NT, preferred_element_type=F32)
+                os[:, lax.rem(b, na_blk) * NB + i, :] = o + pn * kvs[pl.ds(b * NB + i, 1), :kvl]
 
             @pl.when(b + RING < nblk)
             def _():
@@ -217,14 +221,14 @@
             rows = slice((0, na_blk * NB)[half], (na_blk * NB, t)[half])
             nh = rows.stop - rows.start
             for h in range(heads):
-                oc[0:nh, h * vh:(h + 1) * vh] = jnp.dot(os[h, 0:nh].astype(BF), wuv[h], preferred_element_type=F32).astype(BF)
+                oc[:nh, h * vh:(h + 1) * vh] = jnp.dot(os[h, :nh].astype(BF), wuv[h], preferred_element_type=F32).astype(BF)
             ssq = jnp.zeros((nh, 1), F32)
             for a in range(0, hid, 512):
                 h1 = (x_ref[rows, a:a + 512].astype(F32)
-                      + jnp.dot(oc[0:nh], wo[:, a:a + 512], preferred_element_type=F32)).astype(BF)
+                      + jnp.dot(oc[:nh], wo[:, a:a + 512], preferred_element_type=F32)).astype(BF)
                 h1_ref[rows, a:a + 512] = h1
                 hf = h1.astype(F32)
-                ssq = ssq + jnp.sum(hf * hf, axis=1, keepdims=True)
+                ssq = ssq + jnp.sum(hf * hf, axis=LAST, keepdims=YES)
             inv = lax.rsqrt(ssq * (1.0 / hid) + EPS)
             u_all[me, rows, :] = (h1_ref[rows, :].astype(F32) * inv).astype(BF)
             for i in range(rows.start // rsub, rows.stop // rsub):
@@ -263,10 +267,13 @@
             cp.start()
         relay_near(1)
 
+        def act_fn(g, v):
+            return (g * (1.0 / (1.0 + jnp.exp(-g))) * v).astype(BF)
+
         def glu(lhs, gw, uw):
             g = jnp.dot(lhs, gw, preferred_element_type=F32)
             v = jnp.dot(lhs, uw, preferred_element_type=F32)
-            return (g * (1.0 / (1.0 + jnp.exp(-g))) * v).astype(BF)
+            return act_fn(g, v)
 
         def glu_unit(lhs, slot, part_, store):
             width, off = (na, 0) if part_ == 0 else (inter - na, na)
@@ -277,7 +284,11 @@
                 else:
                     buf = wc1 if slot else wc0
                     gw, uw = buf[0, :, a:b], buf[1, :, a:b]
-                store(off + a, off + b, glu(lhs, gw, uw))
+                if b - a == 128:
+                    gv = jnp.dot(lhs, jnp.concatenate([gw, uw], axis=1), preferred_element_type=F32)
+                    store(off + a, off + b, act_fn(gv[:, :LN], gv[:, LN:2 * LN]))
+                else:
+                    store(off + a, off + b, glu(lhs, gw, uw))
 
         for half, part_ in ((0, 0), (1, 0), (0, 1), (1, 1)):
             for cp in load_shared(half, part_, wc1):
@@ -304,23 +315,26 @@
         hit = w_all > 0.0
         rank = jnp.dot(hit.astype(F32).astype(BF), tri, preferred_element_type=F32)
         rank_s[...] = jnp.where(hit, rank, -1000.0).reshape(n, n_loc, 128)
-        row48 = lax.broadcasted_iota(jnp.int32, (2 * CAP, 256), 0).astype(F32)
+        row48 = lax.broadcasted_iota(jnp.int32, (SLOT, 256), 0).astype(F32)
 
         def tables(p, carry):
             for e in range(n_loc):
                 rk = jnp.concatenate([rank_s[2 * p, e:e + 1, :], rank_s[2 * p + 1, e:e + 1, :] + float(CAP)], axis=1)
                 ww = jnp.concatenate([wt_all[2 * p, e:e + 1, :], wt_all[2 * p + 1, e:e + 1, :]], axis=1)
                 sel = row48 == rk
-                pm[p, e * 2 * CAP:(e + 1) * 2 * CAP, :] = jnp.where(sel, 1.0, 0.0).astype(BF)
-                wsel[e * 2 * CAP:(e + 1) * 2 * CAP, :] = jnp.where(sel, ww, 0.0)
+                pm[p, e * SLOT:(e + 1) * SLOT, :] = jnp.where(sel, 1.0, 0.0).astype(BF)
+                wsel[e * SLOT:(e + 1) * SLOT, :] = jnp.where(sel, ww, 0.0)
             wt = wsel[...].T
             b1 = wt.astype(BF)
             r1 = wt - b1.astype(F32)
             b2 = r1.astype(BF)
             b3 = (r1 - b2.astype(F32)).astype(BF)
-            cm[p, 0:256, :] = b1
-            cm[p, 256:512, :] = b2
-            cm[p, 512:768, :] = b3
+            th = t // 2
+            for i, b in enumerate((b1, b2, b3)):
+                for sub in range(2):
+                    for cc in range(2):
+                        r0 = ((sub * 3 + i) * 2 + cc) * th
+                        cm[p, r0:r0 + th, :] = b[cc * t + sub * th:cc * t + (sub + 1) * th]
             return carry
 
         lax.fori_loop(0, 4, tables, 0)
@@ -329,12 +343,12 @@
         relay((6,), dg, (sib,), (1, 2))
 
         def dispatch(p):
-            rows = pl.ds(pl.multiple_of(p * 2 * CAP, 16), 2 * CAP)
+            rows = pl.ds(pl.multiple_of(p * SLOT, 16), SLOT)
             for a in range(0, hid, 512):
                 uv = u_all[pl.ds(2 * p, 2), :, a:a + 512].reshape(256, 512)
                 r = jnp.dot(pm[p], uv, preferred_element_type=F32).astype(BF)
                 for e in range(n_loc):
-                    xr[e, rows, a:a + 512] = r[e * 2 * CAP:(e + 1) * 2 * CAP]
+                    xr[e, rows, a:a + 512] = r[e * SLOT:(e + 1) * SLOT]
 
         arrive(sib)
         dispatch(chip)
@@ -367,9 +381,9 @@
                 load_routed(0, 2 * k + slot).wait()
             outs = [jnp.dot(act[2 * k + slot], wb[2 * k + slot], preferred_element_type=F32).astype(BF) for slot in range(2)]
             for slot, o in enumerate(outs):
-                rows = pl.ds(pl.multiple_of((2 * k + slot) * 2 * CAP, 16), 2 * CAP)
+                rows = pl.ds(pl.multiple_of((2 * k + slot) * SLOT, 16), SLOT)
                 for p in range(4):
-                    orow[p, rows, :] = o[p * 2 * CAP:(p + 1) * 2 * CAP]
+                    orow[p, rows, :] = o[p * SLOT:(p + 1) * SLOT]
 
             @pl.when(k == n_loc // 2 - 2)
             def _():
@@ -390,17 +404,19 @@
         for k in range(1, n):
             wt_copy(k).wait_send()
 
-        def st1(c):
-            return rcopy(part.at[lax.rem(c, 2), 1 - core], rx0.at[lax.rem(c, 4)], d_send.at[0, lax.rem(c, 2)], d_recv.at[0, lax.rem(c, 4)], sib)
-
-        def st2(c):
-            return rcopy(s1.at[lax.rem(c, 2)], rx1.at[lax.rem(c, 4)], d_send.at[1, lax.rem(c, 2)], d_recv.at[1, lax.rem(c, 4)], dev1)
-
-        def st3(c):
-            return rcopy(s2.at[lax.rem(c, 2)], rx2.at[c], d_send.at[2, lax.rem(c, 2)], d_recv.at[2, c], dev2)
-
-        def st4(c):
-            return rcopy(s3.at[lax.rem(c, 2)], rx3.at[c], d_send.at[3, lax.rem(c, 2)], d_recv.at[3, c], sib)
+        th = t // 2
+
+        def st1(q):
+            return rcopy(part.at[lax.rem(q, 2), 1 - core], rx0.at[lax.rem(q, 4)], d_send.at[0, lax.rem(q, 4)], d_recv.at[0, lax.rem(q, 4)], sib)
+
+        def st2(q):
+            return rcopy(s1.at[lax.rem(q, 4)], rx1.at[lax.rem(q, 8)], d_send.at[1, lax.rem(q, 4)], d_recv.at[1, lax.rem(q, 8)], dev1)
+
+        def st3(q):
+            return rcopy(s2.at[lax.rem(q, 4)], rx2.at[q], d_send.at[2, lax.rem(q, 4)], d_recv.at[2, q], dev2)
+
+        def st4(q):
+            return rcopy(s3.at[lax.rem(q, 4)], rx3.at[q], d_send.at[3, lax.rem(q, 4)], d_recv.at[3, q], sib)
 
         def refill(c, grp):
             @pl.when(c + 1 < nc)
@@ -414,23 +430,22 @@
             outs = [jnp.dot(act[e], wb[e], preferred_element_type=F32).astype(BF) for e in grp]
             for e, o in zip(grp, outs):
                 for p in range(4):
-                    orow[p, e * 2 * CAP:(e + 1) * 2 * CAP, :] = o[p * 2 * CAP:(p + 1) * 2 * CAP]
+                    orow[p, e * SLOT:(e + 1) * SLOT, :] = o[p * SLOT:(p + 1) * SLOT]
             refill(c, grp)
 
-        def combine(c):
-            sl = lax.rem(c, 2)
+        def combine(q, sub):
             for dy in (1, 0):
                 for dx in (1, 0):
                     py = (1 - cy) if dy else cy
                     px = (1 - cx) if dx else cx
                     p = py * 2 + px
-                    r3 = jnp.dot(cm[p], orow[p], preferred_element_type=F32)
-                    res = r3[0:256] + r3[256:512] + r3[512:768]
+                    r3 = jnp.dot(cm[p, sub * 6 * th:(sub + 1) * 6 * th, :], orow[p], preferred_element_type=F32)
+                    res = r3[:t] + r3[t:2 * t] + r3[2 * t:3 * t]
                     for h in range(2):
                         a, b = (dx, dy) if h == 0 else (dy, dx)
                         for cc in range(2):
-                            part[sl, h, a, b, cc ^ h] = res[cc * 128:(cc + 1) * 128, h * 128:(h + 1) * 128]
-            st1(c).start()
+                            part[sub, h, a, b, cc ^ h] = res[cc * th:(cc + 1) * th, h * 128:(h + 1) * 128]
+            st1(q).start()
 
         def shared_down(c):
             cols = pl.ds(pl.multiple_of(c * CW, CW), CW)
@@ -444,79 +459,94 @@
 
         def stage2(k):
             sl = lax.rem(k, 2)
+            s4 = lax.rem(k, 4)
             st1(k).wait_recv()
 
-            @pl.when(k >= 2)
+            @pl.when(k >= 4)
             def _():
-                st2(k - 2).wait_send()
+                st2(k - 4).wait_send()
             for b in range(2):
                 for d in range(2):
-                    s1[sl, b, d] = part[sl, core, 1, b, d] + rx0[lax.rem(k, 4), 1, b, d]
+                    s1[s4, b, d] = part[sl, core, 1, b, d] + rx0[s4, 1, b, d]
             st2(k).start()
             for b in range(2):
                 for d in range(2):
-                    keep0[sl, b, d] = part[sl, core, 0, b, d] + rx0[lax.rem(k, 4), 0, b, d]
+                    keep0[s4, b, d] = part[sl, core, 0, b, d] + rx0[s4, 0, b, d]
             st1(k).wait_send()
 
         def stage3(k):
-            sl = lax.rem(k, 2)
+            s4 = lax.rem(k, 4)
             st2(k).wait_recv()
 
-            @pl.when(k >= 2)
+            @pl.when(k >= 4)
             def _():
-                st3(k - 2).wait_send()
+                st3(k - 4).wait_send()
             for d in range(2):
-                s2[sl, d] = keep0[sl, 1, d] + rx1[lax.rem(k, 4), 1, d]
+                s2[s4, d] = keep0[s4, 1, d] + rx1[lax.rem(k, 8), 1, d]
             st3(k).start()
             for d in range(2):
-                keep1[sl, d] = keep0[sl, 0, d] + rx1[lax.rem(k, 4), 0, d]
+                keep1[s4, d] = keep0[s4, 0, d] + rx1[lax.rem(k, 8), 0, d]
 
         def stage4(k):
-            sl = lax.rem(k, 2)
+            s4 = lax.rem(k, 4)
             st3(k).wait_recv()
 
-            @pl.when(k >= 2)
+            @pl.when(k >= 4)
             def _():
-                st4(k - 2).wait_send()
-            s3[sl] = keep1[sl, 1] + rx2[k, 1]
+                st4(k - 4).wait_send()
+            s3[s4] = keep1[s4, 1] + rx2[k, 1]
             st4(k).start()
-            keep2[sl] = keep1[sl, 0] + rx2[k, 0]
+            keep2[s4] = keep1[s4, 0] + rx2[k, 0]
 
         def stage5(k):
-            mine = pl.ds(pl.multiple_of(k * CW + core * 128, 128), 128)
-            other = pl.ds(pl.multiple_of(k * CW + (1 - core) * 128, 128), 128)
+            c = k // 2
+            mine = pl.ds(pl.multiple_of(c * CW + core * 128, 128), 128)
+            other = pl.ds(pl.multiple_of(c * CW + (1 - core) * 128, 128), 128)
+            rows = pl.ds(pl.multiple_of(lax.rem(k, 2) * th, th), th)
             st4(k).wait_recv()
-            y_ref[:, mine] = (ybase[:, mine] + keep2[lax.rem(k, 2)]).astype(BF)
-            y_ref[:, other] = (ybase[:, other] + rx3[k]).astype(BF)
+            y_ref[rows, mine] = (ybase[rows, mine] + keep2[lax.rem(k, 4)]).astype(BF)
+            y_ref[rows, other] = (ybase[rows, other] + rx3[k]).astype(BF)
+
+        nq2 = 2 * nc
+
+        def pipe(lag, fn, q):
+            pl.when(jnp.logical_and(q >= lag, q < nq2 + lag))(lambda: fn(q - lag))
 
         def chunk(c, carry):
             live = c < nc
+            q = 2 * c
             pl.when(jnp.logical_and(c >= 1, live))(lambda: down(c, (0, 1, 2, 3)))
-            pl.when(jnp.logical_and(c >= 1, c < nc + 1))(lambda: stage2(c - 1))
+            pipe(1, stage2, q)
             pl.when(jnp.logical_and(c >= 1, live))(lambda: down(c, (4, 5, 6, 7)))
-            pl.when(live)(lambda: combine(c))
+            pl.when(live)(lambda: combine(q, 0))
+            pipe(3, stage3, q)
+            pipe(5, stage4, q)
+            pipe(6, stage5, q)
+            q = 2 * c + 1
+            pl.when(live)(lambda: combine(q, 1))
+            pipe(1, stage2, q)
             pl.when(live)(lambda: shared_down(c))
-            pl.when(jnp.logical_and(c >= 2, c < nc + 2))(lambda: stage3(c - 2))
-            pl.when(jnp.logical_and(c >= 3, c < nc + 3))(lambda: stage4(c - 3))
-            pl.when(c >= 4)(lambda: stage5(c - 4))
+            pipe(3, stage3, q)
+            pipe(5, stage4, q)
+            pipe(6, stage5, q)
             return carry
 
-        lax.fori_loop(0, nc + 4, chunk, 0)
-        for k in (nc - 2, nc - 1):
+        lax.fori_loop(0, nc + 3, chunk, 0)
+        for k in range(nq2 - 4, nq2):
             st2(k).wait_send()
             st3(k).wait_send()
             st4(k).wait_send()
 
     pl.run_scoped(
         moe_scope,
-        V((n, n_loc, t), F32), V((n_loc * 2 * CAP, 256), F32),
-        V((4, n_loc * 2 * CAP, 256), BF), V((4, 768, n_loc * 2 * CAP), BF),
+        V((n, n_loc, t), F32), V((n_loc * SLOT, 256), F32),
+        V((4, n_loc * SLOT, 256), BF), V((4, 768, n_loc * SLOT), BF),
         V((n_loc, 8 * CAP, hid), BF), V((n_loc, 8 * CAP, inter), BF), V((t, 2 * inter), BF),
-        V((4, n_loc * 2 * CAP, CW), BF),
+        V((4, n_loc * SLOT, CW), BF),
         V((2, hid, inter - NA), BF), V((n_loc + 2, inter, CW), BF), V((t, hid), F32),
-        V((2, 2, 2, 2, 2, t, 128), F32),
-        V((2, 2, 2, t, 128), F32), V((2, 2, 2, t, 128), F32),
-        V((2, 2, t, 128), F32), V((2, 2, t, 128), F32), V((2, t, 128), F32), V((2, t, 128), F32))
+        V((2, 2, 2, 2, 2, t // 2, LN), F32),
+        V((4, 2, 2, t // 2, LN), F32), V((4, 2, 2, t // 2, LN), F32),
+        V((4, 2, t // 2, LN), F32), V((4, 2, t // 2, LN), F32), V((4, t // 2, LN), F32), V((4, t // 2, LN), F32))
 
 
 def copy_kernel(a_ref, b_ref, y_ref, kv_ref):
@@ -532,10 +562,7 @@
     nc = hid // CW
     rot = kvd - kvl
     half = rot // 2
-    lane = jnp.arange(128)
-    ang = ((lens[:, None] * 128 + lane[None, :]) >> 7).astype(F32) * (ROPE_BASE ** (-2.0 * (lane % half).astype(F32) / rot))[None, :]
-    cs4 = jnp.cos(ang)
-    sn4 = jnp.sin(ang) * jnp.where(lane % rot < half, -1.0, 1.0)[None, :]
+    inv = np.tile(ROPE_BASE ** (-2.0 * np.arange(half) / rot), 128 // half)[None, :].astype(np.float32)
     V = pltpu.VMEM
     D = pltpu.SemaphoreType.DMA
     vm = pl.BlockSpec(memory_space=pltpu.VMEM)
@@ -548,13 +575,14 @@
         scratch_shapes=[
             V((8, t, hid), BF), V((8 * n_loc, t), F32), V((8, n_loc, t), F32), V((t, hid), BF),
             V((4, hid, NA), BF), V((2, hid, e_gate.shape[2] - NA), BF),
-            V((4, 2, 2, 2, t, 128), F32), V((4, 2, 2, t, 128), F32), V((nc, 2, t, 128), F32), V((nc, t, 128), F32),
+            V((4, 2, 2, 2, t // 2, LN), F32), V((8, 2, 2, t // 2, LN), F32),
+            V((2 * nc, 2, t // 2, LN), F32), V((2 * nc, t // 2, LN), F32),
             D((4,)), D((heads // 4,)), D((RING,)), D((2, 2, 2)), D((n_loc + 2,)), D((8,)), D((8,)),
-            D((7, NSUB)), D((8, NSUB)), D((4, 2)), D((4, nc)),
+            D((7, NSUB)), D((8, NSUB)), D((4, 4)), D((4, 2 * nc)),
         ],
         compiler_params=pltpu.CompilerParams(collective_id=0, has_side_effects=True, vmem_limit_bytes=67043328),
         name='layer',
-    )(lens, ids.T, rw.T, x, cs4, sn4, w_q, w_dkv.T, w_uk, w_uv, w_o, cache.transpose(0, 2, 1),
+    )(lens, lens.reshape(1, t), jnp.asarray(inv), ids.T, rw.T, x, w_q, w_dkv.T, w_uk, w_uv, w_o, cache.transpose(0, 2, 1),
       s_gate, s_up, s_down, e_gate, e_up, e_down)
     y, kvt = pl.pallas_call(
         copy_kernel,

time: 124 us -> 121 us (0.976)
  other arithmetic: 1.65 us -> 0 us
    mul x2 -> x0, other arithmetic: 1.64 us -> none  [the longest x1 0.98 us: layer(): sn4 = jnp.sin(ang) * jnp.where(lane % rot < half, -1.0, 1.0)[None, :]]
where the time goes in v4:
time: 121 us
  Pallas kernels  120 us (99%)
    pallas_call x1, Pallas kernels, layer(): pl.pallas_call(layer_kernel, out_shape=(jax.ShapeDtypeStruct((t, hid), BF...  118 us

profile of v4, /device:TPU:0, one launch (start us, length us, event | category | flops | bytes accessed | tf_op | source)
XLA Modules:
  0.0 120.7 jit_solution(13010223609028182611)
XLA Ops:
  0.6 118.1 %layer.1 = (bf16[128,2048]{1,0:T(8,128)(2,1)}, bf16[576,128]{1,0:T(8,128)(2,1)}) custom-call(s32[128]{0:T(128)} %lens_ref.1, s32[1,128]{1,0:T(1,128)} %bitcast.10, f32[1,128]{1,0:T(1,128)} %constant.2.clone.inv_ref, s32[6,128]{1,0:T(8,128)} %bitcast.8, f32[6,128]{1,0:T(8,128)} %bitcast.9, bf16[128,2048]{1,0:T(8,128)(2,1)} %x_ref.1, bf16[2048,3072]{1,0:T(8,128)(2,1)} %wq_h.1, ...), custom_call_target="tpu_custom_call" | custom-call | tf_op jit(solution)/shard_map/layer/pallas_call | solution.py:570
  118.7 1.9 %out.1 = (bf16[128,2048]{1,0:T(8,128)(2,1)}, bf16[576,128]{1,0:T(8,128)(2,1)}) custom-call(bf16[128,2048]{1,0:T(8,128)(2,1)} %get-tuple-element.6.a_ref, bf16[576,128]{1,0:T(8,128)(2,1)} %get-tuple-element.7.b_ref), custom_call_target="tpu_custom_call" | custom-call | tf_op jit(solution)/shard_map/out/pallas_call | solution.py:587
